TPU v7x, 32 devices: a whole 2x2x4 slice. The times are simulated.
32 devices in a mesh: cell: 8 (over z, x), gene: 4 (over y, core).
Axes of the slice: x: 2, y: 2, z: 4, core: 2. Of those that a mesh axis runs over, the one named last changes fastest.
Arguments:
- counts: int32 [2048, 4096], P('cell', 'gene'), may hold values from 0 to 7
- totals: int32 [2048], P('cell'), may hold values from 1000 to 19999
- cell_factors: float32 [2048, 32], P('cell'), may hold values from -0.9 to 0.9
- gene_loadings: float32 [4096, 32], P('gene'), may hold values from -0.9 to 0.9
Outputs:
- new_factors: float32 [2048, 32], P('cell')
- new_loadings: float32 [4096, 32], P('gene')
- deviance: float32 [4096], P('gene')
All inputs are finite; a program needn't handle non-finite values.
Results may differ from a plain program's by a relative error of at most 0.0044.
Values sent between devices are 32-bit elements; how exact they have to be, the bound alone decides.
No kernel may reach another device: no remote copies, remote signals or barrier semaphores. Data moves between devices by JAX's collectives and lax.ppermute only.
A program may use at most 128 MiB of HBM per device.

v0:
```python
import functools
import math

import jax
import jax.numpy as jnp
from jax import lax
from jax.experimental import pallas as pl
from jax.experimental.pallas import tpu as pltpu
from jax.sharding import PartitionSpec as P


RIDGE = 1.0
DAMPING = 0.1
SCALE_TOTAL = 5000.0
SUB = 8
MIB = 1024 * 1024


def table_pieces(width):
    return [(a, q) for a in range(width) for q in range(a // SUB, width // SUB)]


def fill_table(table_ref, x, width):
    pieces = table_pieces(width)
    chunks = [x[SUB * q : SUB * q + SUB] for q in range(width // SUB)]
    for p in range(0, len(pieces), 2):
        pair = [x[a : a + 1] * chunks[q] for a, q in pieces[p : p + 2]]
        table_ref[SUB * p : SUB * (p + 2)] = jnp.concatenate(pair, axis=0).astype(jnp.bfloat16)


def three(x):
    high = x.astype(jnp.bfloat16)
    rest = x - high.astype(jnp.float32)
    mid = rest.astype(jnp.bfloat16)
    low = (rest - mid.astype(jnp.float32)).astype(jnp.bfloat16)
    return high, mid, low


def pad_rows(rows):
    index = lax.broadcasted_iota(jnp.int32, (16, rows[0].shape[1]), 0)
    total = jnp.zeros((16, rows[0].shape[1]), jnp.float32)
    for k, row in enumerate(rows):
        total = jnp.where(index == k, row.astype(jnp.float32), total)
    return total.astype(jnp.bfloat16)


def stack_left(x, offset):
    high, mid, low = three(x)
    return jnp.concatenate([high, mid, high, low, mid, high, pad_rows(list(three(offset)))], axis=0)


def stack_right(y):
    high, mid, low = three(y)
    ones = pad_rows([jnp.ones((1, y.shape[1]), jnp.float32)] * 3)
    return jnp.concatenate([high, high, mid, high, mid, low, ones], axis=0)


def cholesky_columns(get, put, width, lanes):
    blocks = width // SUB
    index = lax.broadcasted_iota(jnp.int32, (SUB, lanes), 0)
    trace = jnp.zeros((SUB, lanes), jnp.float32)
    for k in range(width):
        trace = trace + jnp.where(index == k % SUB, get(k, k // SUB), 0.0)
    shift = RIDGE + DAMPING / width * jnp.sum(trace, axis=0, keepdims=True)
    scales = []
    columns = []
    for k in range(width):
        first = k // SUB
        column = {q: get(k, q) for q in range(first, blocks)}
        column[first] = column[first] + jnp.where(index == k % SUB, shift, 0.0)
        for m in range(k):
            factor = columns[m][first][k % SUB : k % SUB + 1]
            for q in range(first, blocks):
                column[q] = column[q] - columns[m][q] * factor
        scale = lax.rsqrt(column[first][k % SUB : k % SUB + 1])
        column = {q: v * scale for q, v in column.items()}
        for q, v in column.items():
            put(k, q, v)
        columns.append(column)
        scales.append(scale)
    return columns, scales


def cholesky_substitute(columns, scales, right, width, lanes):
    blocks = width // SUB
    index = lax.broadcasted_iota(jnp.int32, (SUB, lanes), 0)
    right = list(right)
    forward = []
    for k in range(width):
        first = k // SUB
        value = right[first][k % SUB : k % SUB + 1] * scales[k]
        forward.append(value)
        for q in range(first, blocks):
            right[q] = right[q] - columns[k][q] * value
    answer = [jnp.zeros((SUB, lanes), jnp.float32)] * blocks
    for k in reversed(range(width)):
        first = k // SUB
        terms = sum(columns[k][q] * answer[q] for q in range(first, blocks))
        value = (forward[k] - jnp.sum(terms, axis=0, keepdims=True)) * scales[k]
        answer[first] = jnp.where(index == k % SUB, value, answer[first])
    return answer


def factor_moments_kernel(width, counts_ref, totals_ref, ut_ref, vt_ref, mine_ref, theirs_ref, keep_ref, table_ref):
    half = ut_ref.shape[1] // 2
    core = lax.rem(lax.axis_index("gene"), 2)
    parts = (pl.multiple_of(core * half, half), pl.multiple_of((1 - core) * half, half))
    offset = jnp.log(totals_ref[...].astype(jnp.float32)) - math.log(SCALE_TOTAL)
    keep_ref[...] = jnp.zeros_like(keep_ref)
    keep_ref[0:1] = offset
    vt = vt_ref[...]
    fill_table(table_ref, vt, width)
    right = stack_right(vt)
    low = vt.astype(jnp.bfloat16)
    across = (((1,), (1,)), ((), ()))
    for part, out_ref in zip(parts, (mine_ref, theirs_ref)):
        left = stack_left(ut_ref[:, pl.ds(part, half)], keep_ref[0:1, pl.ds(part, half)])
        linear = lax.dot_general(
            left, right, (((0,), (0,)), ((), ())), preferred_element_type=jnp.float32
        )
        expected = jnp.exp(linear)
        weights = expected.astype(jnp.bfloat16)
        counts = counts_ref[pl.ds(part, half), :].astype(jnp.float32)
        residual = (counts - expected).astype(jnp.bfloat16)
        rows = table_ref.shape[0]
        out_ref[:rows] = lax.dot_general(table_ref[...], weights, across, preferred_element_type=jnp.float32)
        out_ref[rows:] = lax.dot_general(low, residual, across, preferred_element_type=jnp.float32)


def factor_solve_kernel(width, own_ref, other_ref, totals_ref, ut_ref, new_ref):
    half = own_ref.shape[1]
    core = lax.rem(lax.axis_index("gene"), 2)
    part = pl.multiple_of(core * half, half)
    pieces = table_pieces(width)
    place = {piece: SUB * p for p, piece in enumerate(pieces)}
    base = SUB * len(pieces)

    def get(a, q):
        at = place[a, q]
        return own_ref[at : at + SUB, :] + other_ref[at : at + SUB, :]

    ut = ut_ref[:, pl.ds(part, half)]
    right = []
    for q in range(width // SUB):
        at = base + SUB * q
        gradient = own_ref[at : at + SUB, :] + other_ref[at : at + SUB, :]
        right.append(gradient - RIDGE * ut[SUB * q : SUB * q + SUB])
    columns, scales = cholesky_columns(get, lambda a, q, v: None, width, half)
    step = cholesky_substitute(columns, scales, right, width, half)
    offset = jnp.log(totals_ref[:, pl.ds(part, half)].astype(jnp.float32)) - math.log(SCALE_TOTAL)
    new_ref[...] = jnp.zeros_like(new_ref)
    for q in range(width // SUB):
        new_ref[0, SUB * q : SUB * q + SUB, :] = ut[SUB * q : SUB * q + SUB] + step[q]
    new_ref[0, width : width + 1, :] = offset


def counts_kernel(width, counts_ref, mine_ref, theirs_ref, vt_ref, factors_ref, linear_ref):
    half = mine_ref.shape[2]
    core = lax.rem(lax.axis_index("gene"), 2)
    total = jnp.zeros((width, counts_ref.shape[1]), jnp.float32)
    terms = jnp.zeros((1, counts_ref.shape[1]), jnp.float32)
    for own, block_ref in ((1, mine_ref), (0, theirs_ref)):
        index = core if own else 1 - core
        part = pl.multiple_of(index * half, half)
        block = block_ref[0]
        factors = block[:width]
        factors_ref[:, pl.ds(part, half)] = factors
        counts = counts_ref[pl.ds(part, half), :].astype(jnp.float32)
        exact = counts.astype(jnp.bfloat16)
        high, mid, low = three(factors)
        both = jnp.concatenate([high, mid, low], axis=0)
        product = jnp.dot(both, exact, preferred_element_type=jnp.float32)
        total = total + product[:width]
        full = product[:width] + (product[width : 2 * width] + product[2 * width :])
        terms = terms - jnp.sum(full * vt_ref[...], axis=0, keepdims=True)
        oh, om, ol = three(block[width : width + 1])
        offsets = jnp.dot(pad_rows([oh, om, ol]), exact, preferred_element_type=jnp.float32)
        own_terms = counts * (jnp.log(jnp.maximum(counts, 1.0)) - 1.0)
        terms = terms + jnp.sum(own_terms, axis=0, keepdims=True)
        terms = terms - jnp.sum(offsets[:SUB], axis=0, keepdims=True)
    linear_ref[:width] = total
    linear_ref[width:] = jnp.zeros_like(linear_ref[width:])
    linear_ref[width : width + 1] = terms


def loading_moments_kernel(width, per, tile, blocks_ref, vt_ref, out_ref, sum_ref, table_ref, left_ref, right_ref):
    genes = vt_ref.shape[1]
    half = blocks_ref.shape[2]
    groups = blocks_ref.shape[0] // per
    rows = SUB * len(table_pieces(width))
    right_ref[...] = stack_right(vt_ref[...])
    if groups > 1:
        out_ref[...] = jnp.zeros_like(out_ref)
        sum_ref[...] = jnp.zeros_like(sum_ref)

    @pl.loop(0, groups)
    def _(group):
        for b in range(per):
            block = blocks_ref[group * per + b]
            factors = block[:width]
            cols = slice(b * half, (b + 1) * half)
            fill_table(table_ref.at[:, cols], factors, width)
            table_ref[rows : rows + width, cols] = factors.astype(jnp.bfloat16)
            left_ref[:, cols] = stack_left(factors, block[width : width + 1])

        @pl.loop(0, genes // tile)
        def _(j):
            at = pl.ds(pl.multiple_of(j * tile, tile), tile)
            linear = lax.dot_general(
                left_ref[...], right_ref[:, at], (((0,), (0,)), ((), ())), preferred_element_type=jnp.float32
            )
            expected = jnp.exp(linear)
            total = jnp.sum(expected, axis=0, keepdims=True)
            product = jnp.dot(table_ref[...], expected.astype(jnp.bfloat16), preferred_element_type=jnp.float32)
            if groups > 1:
                sum_ref[0:1, at] += total
                out_ref[:, at] += product
            else:
                sum_ref[0:1, at] = total
                out_ref[:, at] = product


def loading_factor_kernel(width, tile, moments_ref, more_ref, lower_ref, scale_ref):
    genes = moments_ref.shape[1]
    place = {piece: SUB * p for p, piece in enumerate(table_pieces(width))}

    @pl.loop(0, genes // tile)
    def _(j):
        at = pl.ds(pl.multiple_of(j * tile, tile), tile)

        def get(a, q):
            rows = slice(place[a, q], place[a, q] + SUB)
            return moments_ref[rows, at] + more_ref[rows, at]

        def put(a, q, value):
            lower_ref[place[a, q] : place[a, q] + SUB, at] = value

        _, scales = cholesky_columns(get, put, width, tile)
        for k in range(width):
            scale_ref[k : k + 1, at] = scales[k]


def loading_solve_kernel(width, tile, total_cells, lower_ref, scale_ref, moments_ref, more_ref, sum_ref, sums_ref, own_ref, other_ref, vt_ref, new_ref, deviance_ref):
    genes = vt_ref.shape[1]
    place = {piece: SUB * p for p, piece in enumerate(table_pieces(width))}
    base = SUB * len(place)
    blocks = width // SUB

    @pl.loop(0, genes // tile)
    def _(j):
        at = pl.ds(pl.multiple_of(j * tile, tile), tile)
        right = []
        for q in range(blocks):
            rows = slice(SUB * q, SUB * q + SUB)
            expected = moments_ref[base + SUB * q : base + SUB * q + SUB, at]
            expected = expected + more_ref[base + SUB * q : base + SUB * q + SUB, at]
            right.append(own_ref[rows, at] + other_ref[rows, at] - expected - RIDGE * vt_ref[rows, at])
        columns = [
            {q: lower_ref[place[k, q] : place[k, q] + SUB, at] for q in range(k // SUB, blocks)} for k in range(width)
        ]
        scales = [scale_ref[k : k + 1, at] for k in range(width)]
        step = cholesky_substitute(columns, scales, right, width, tile)
        for q in range(blocks):
            rows = slice(SUB * q, SUB * q + SUB)
            new_ref[rows, at] = vt_ref[rows, at] + step[q]
        last = slice(width, width + 1)
        fixed = own_ref[last, at] + other_ref[last, at] + sum_ref[0:1, at] + sums_ref[0:1, at]
        deviance_ref[:, at] = fixed * (2.0 / total_cells)


def kernel_call(body, outs, scratch, flops, limit=8):
    single = pl.BlockSpec(memory_space=pltpu.VMEM)

    def call(*args):
        return pl.pallas_call(
            body,
            out_shape=outs,
            in_specs=[single] * len(args),
            out_specs=jax.tree.map(lambda _: single, outs),
            scratch_shapes=scratch,
            compiler_params=pltpu.CompilerParams(vmem_limit_bytes=limit * MIB),
            cost_estimate=pl.CostEstimate(flops=flops, bytes_accessed=1 << 20, transcendentals=0),
        )(*args)

    return call


def exchange(x, axis, bit):
    size = lax.axis_size(axis)
    return lax.ppermute(x, axis, [(i, i ^ bit) for i in range(size)])


def sweep(counts, totals, cell_factors, gene_loadings):
    cells, genes = counts.shape
    width = cell_factors.shape[1]
    half = cells // 2
    rows = SUB * len(table_pieces(width))
    shape = functools.partial(jax.ShapeDtypeStruct, dtype=jnp.float32)
    tall = width + SUB
    ut, vt = cell_factors.T, gene_loadings.T
    totals = totals.reshape(1, cells)

    mine, theirs = kernel_call(
        functools.partial(factor_moments_kernel, width),
        (shape((rows + width, half)), shape((rows + width, half))),
        [pltpu.VMEM((SUB, cells), jnp.float32), pltpu.VMEM((rows, genes), jnp.bfloat16)],
        10**9,
    )(counts, totals, ut, vt)
    mine = mine + exchange(theirs, "gene", 1)
    bits = [1 << k for k in range(1, (lax.axis_size("gene") - 1).bit_length())]
    for bit in bits[:-1]:
        mine = mine + exchange(mine, "gene", bit)
    other = exchange(mine, "gene", bits[-1])
    block = kernel_call(
        functools.partial(factor_solve_kernel, width), shape((1, tall, half)), [], 10**9
    )(mine, other, totals, ut)

    cell_bits = [1 << k for k in range((lax.axis_size("cell") - 1).bit_length())]
    gathered = block
    for bit in reversed(cell_bits):
        gathered = jnp.concatenate([gathered, exchange(gathered, "cell", bit)], axis=0)
    partner = exchange(block, "gene", 1)
    opposite = exchange(gathered, "gene", 1)

    factors, linear = kernel_call(
        functools.partial(counts_kernel, width), (shape((width, cells)), shape((tall, genes))), [], 10**9
    )(counts, block, partner, vt)
    for bit in cell_bits[:-1]:
        linear = linear + exchange(linear, "cell", bit)
    linear_other = exchange(linear, "cell", cell_bits[-1])

    per = min(gathered.shape[0], 8)
    tile = 256
    depth = 6 * width + 16

    def moments_of(blocks):
        return kernel_call(
            functools.partial(loading_moments_kernel, width, per, tile),
            (shape((rows + width, genes)), shape((SUB, genes))),
            [
                pltpu.VMEM((rows + width, per * half), jnp.bfloat16),
                pltpu.VMEM((depth, per * half), jnp.bfloat16),
                pltpu.VMEM((depth, genes), jnp.bfloat16),
            ],
            4 * 10**9,
            16,
        )(blocks, vt)

    moments, sums = moments_of(gathered)
    more, more_sums = moments_of(opposite)
    lower, scales = kernel_call(
        functools.partial(loading_factor_kernel, width, 256),
        (shape((rows, genes)), shape((width, genes))),
        [],
        4 * 10**9,
    )(moments, more)
    total_cells = cells * lax.axis_size("cell")
    new_loadings, deviance = kernel_call(
        functools.partial(loading_solve_kernel, width, min(genes, 1024), total_cells),
        (shape((width, genes)), shape((1, genes))),
        [],
        10**9,
    )(lower, scales, moments, more, sums, more_sums, linear, linear_other, vt)
    return (factors.T, new_loadings.T, deviance.reshape(genes))


def solution(mesh):
    return jax.shard_map(
        sweep,
        mesh=mesh,
        in_specs=(P("cell", "gene"), P("cell"), P("cell", None), P("gene", None)),
        out_specs=(P("cell", None), P("gene", None), P("gene")),
        check_vma=False,
    )
```

profile of v0, /device:TPU:0, one launch (start us, length us, event | category | flops | bytes accessed | tf_op | source)
XLA Modules:
  0.0 57.0 jit_solution(10360559624342474860)
XLA Ops:
  0.7 0.9 %copy-done = f32[1024,32]{0,1:T(8,128)S(1)} copy-done((f32[1024,32]{0,1:T(8,128)S(1)}, f32[1024,32]{0,1:T(8,128)}, u32[]{:S(2)}) %copy-start) | copy-done | bytes 131096
  1.6 1.2 %copy-done.2 = s32[256,1024]{1,0:T(8,128)S(1)} copy-done((s32[256,1024]{1,0:T(8,128)S(1)}, s32[256,1024]{1,0:T(8,128)}, u32[]{:S(2)}) %copy-start.2) | copy-done | bytes 1048600
  2.8 0.8 %copy-done.4 = f32[256,32]{0,1:T(8,128)S(1)} copy-done((f32[256,32]{0,1:T(8,128)S(1)}, f32[256,32]{0,1:T(8,128)}, u32[]{:S(2)}) %copy-start.4) | copy-done | bytes 32792
  3.5 0.7 %copy-done.6 = s32[256]{0:T(256)S(1)} copy-done((s32[256]{0:T(256)S(1)}, s32[256]{0:T(256)}, u32[]{:S(2)}) %copy-start.6) | copy-done | bytes 1048
  4.2 1.3 %shard_map.67 = (f32[672,128]{1,0:T(8,128)S(1)}, f32[672,128]{1,0:T(8,128)S(1)}) custom-call(s32[256,1024]{1,0:T(8,128)S(1)} %copy-done.2, s32[1,256]{1,0:T(1,128)S(1)} %bitcast.13, f32[32,256]{1,0:T(8,128)S(1)} %bitcast.11, f32[32,1024]{1,0:T(8,128)S(1)} %bitcast.6), custom_call_target="tpu_custom_call" | custom-call | flops 1000000000 | bytes 1048576 | tf_op jit(solution)/shard_map/pallas_call | solution.py:275
  6.1 1.3 %collective-permute-done = f32[672,128]{1,0:T(8,128)S(1)} collective-permute-done((f32[672,128]{1,0:T(8,128)S(1)}, f32[672,128]{1,0:T(8,128)S(1)}, u32[]{:S(2)}, u32[]{:S(2)}) %collective-permute-start) | collective-permute-done | bytes 344096 | tf_op jit(solution)/shard_map/ppermute | solution.py:290
  7.4 2.9 %collective-permute-start.1 = (f32[672,128]{1,0:T(8,128)S(1)}, f32[672,128]{1,0:T(8,128)S(1)}, u32[]{:S(2)}, u32[]{:S(2)}) collective-permute-start(f32[672,128]{1,0:T(8,128)S(1)} %add.9.own_ref), channel_id=1, source_target_pairs={{0,2},{1,3},{2,0},{3,1},{4,6},{5,7},{6,4},{7,5},{8,10},{9,11},{10,... | collective-permute-start | bytes 1032200 | tf_op jit(solution)/shard_map/ppermute | solution.py:290
  10.4 8.4 %collective-permute-done.1.other_ref = f32[672,128]{1,0:T(8,128)S(1)} collective-permute-done((f32[672,128]{1,0:T(8,128)S(1)}, f32[672,128]{1,0:T(8,128)S(1)}, u32[]{:S(2)}, u32[]{:S(2)}) %collective-permute-start.1) | collective-permute-done | bytes 344096 | tf_op jit(solution)/shard_map/ppermute | solution.py:290
  18.7 0.9 %shard_map.68.mine_ref = f32[1,40,128]{2,1,0:T(8,128)S(1)} custom-call(f32[672,128]{1,0:T(8,128)S(1)} %add.9.own_ref, f32[672,128]{1,0:T(8,128)S(1)} %collective-permute-done.1.other_ref, s32[1,256]{1,0:T(1,128)S(1)} %bitcast.14, f32[32,256]{1,0:T(8,128)S(1)} %bitcast.12), custom_call_target="tpu_custom_call" | custom-call | flops 1000000000 | bytes 1048576 | tf_op jit(solution)/shard_map/pallas_call | solution.py:275
  19.6 2.9 %collective-permute-start.3 = (f32[1,40,128]{2,1,0:T(8,128)S(1)}, f32[1,40,128]{2,1,0:T(8,128)S(1)}, u32[]{:S(2)}, u32[]{:S(2)}) collective-permute-start(f32[1,40,128]{2,1,0:T(8,128)S(1)} %shard_map.68.mine_ref), channel_id=1, source_target_pairs={{0,16},{4,20},{8,24},{12,28},{16,0},{20,4},{24,8},{28,12},{1,17},{... | collective-permute-start | bytes 61448 | tf_op jit(solution)/shard_map/ppermute | solution.py:290
  22.5 1.9 %collective-permute-done.3 = f32[1,40,128]{2,1,0:T(8,128)S(1)} collective-permute-done((f32[1,40,128]{2,1,0:T(8,128)S(1)}, f32[1,40,128]{2,1,0:T(8,128)S(1)}, u32[]{:S(2)}, u32[]{:S(2)}) %collective-permute-start.3) | collective-permute-done | bytes 20512 | tf_op jit(solution)/shard_map/ppermute | solution.py:290
  24.4 1.8 %collective-permute-start.4 = (f32[2,40,128]{2,1,0:T(8,128)S(1)}, f32[2,40,128]{2,1,0:T(8,128)S(1)}, u32[]{:S(2)}, u32[]{:S(2)}) collective-permute-start(f32[2,40,128]{2,1,0:T(8,128)S(1)} %pad_maximum_fusion.2), channel_id=1, source_target_pairs={{0,8},{4,12},{8,0},{12,4},{16,24},{20,28},{24,16},{28,20},{1,9},{5... | collective-permute-start | bytes 122888 | tf_op jit(solution)/shard_map/ppermute | solution.py:290
  26.2 2.2 %collective-permute-done.4 = f32[2,40,128]{2,1,0:T(8,128)S(1)} collective-permute-done((f32[2,40,128]{2,1,0:T(8,128)S(1)}, f32[2,40,128]{2,1,0:T(8,128)S(1)}, u32[]{:S(2)}, u32[]{:S(2)}) %collective-permute-start.4) | collective-permute-done | bytes 40992 | tf_op jit(solution)/shard_map/ppermute | solution.py:290
  28.4 1.7 %collective-permute-start.5 = (f32[4,40,128]{2,1,0:T(8,128)S(1)}, f32[4,40,128]{2,1,0:T(8,128)S(1)}, u32[]{:S(2)}, u32[]{:S(2)}) collective-permute-start(f32[4,40,128]{2,1,0:T(8,128)S(1)} %pad_maximum_fusion.1), channel_id=1, source_target_pairs={{0,4},{4,0},{8,12},{12,8},{16,20},{20,16},{24,28},{28,24},{1,5},{5... | collective-permute-start | bytes 245768 | tf_op jit(solution)/shard_map/ppermute | solution.py:290
  30.1 1.0 %shard_map.69 = (f32[32,256]{1,0:T(8,128)}, f32[40,1024]{1,0:T(8,128)S(1)}) custom-call(s32[256,1024]{1,0:T(8,128)S(1)} %copy-done.3, f32[1,40,128]{2,1,0:T(8,128)S(1)} %shard_map.68.mine_ref, f32[1,40,128]{2,1,0:T(8,128)S(1)} %collective-permute-done.2.theirs_ref, f32[32,1024]{1,0:T(8,128)S(1)} %bitcast.7), custom_call_target="tpu_custom_call" | custom-call | flops 1000000000 | bytes 1048576 | tf_op jit(solution)/shard_map/pallas_call | solution.py:275
  31.5 2.2 %collective-permute-done.5 = f32[4,40,128]{2,1,0:T(8,128)S(1)} collective-permute-done((f32[4,40,128]{2,1,0:T(8,128)S(1)}, f32[4,40,128]{2,1,0:T(8,128)S(1)}, u32[]{:S(2)}, u32[]{:S(2)}) %collective-permute-start.5) | collective-permute-done | bytes 81952 | tf_op jit(solution)/shard_map/ppermute | solution.py:290
  33.8 4.2 %shard_map.70 = (f32[672,1024]{1,0:T(8,128)S(1)}, f32[8,1024]{1,0:T(8,128)S(1)}) custom-call(f32[8,40,128]{2,1,0:T(8,128)S(1)} %pad_maximum_fusion.blocks_ref, f32[32,1024]{1,0:T(8,128)S(1)} %bitcast.8), custom_call_target="tpu_custom_call" | custom-call | flops 4000000000 | bytes 1048576 | tf_op jit(solution)/shard_map/pallas_call | solution.py:275
  38.1 1.1 %collective-permute-start.8 = (f32[40,1024]{1,0:T(8,128)S(1)}, f32[40,1024]{1,0:T(8,128)S(1)}, u32[]{:S(2)}, u32[]{:S(2)}) collective-permute-start(f32[40,1024]{1,0:T(8,128)S(1)} %add.10), channel_id=1, source_target_pairs={{0,8},{4,12},{8,0},{12,4},{16,24},{20,28},{24,16},{28,20},{1,9},{5... | collective-permute-start | bytes 491528 | tf_op jit(solution)/shard_map/ppermute | solution.py:290
  39.2 4.2 %shard_map.71 = (f32[672,1024]{1,0:T(8,128)S(1)}, f32[8,1024]{1,0:T(8,128)S(1)}) custom-call(f32[8,40,128]{2,1,0:T(8,128)S(1)} %collective-permute-done.6.blocks_ref, f32[32,1024]{1,0:T(8,128)S(1)} %bitcast.9), custom_call_target="tpu_custom_call" | custom-call | flops 4000000000 | bytes 1048576 | tf_op jit(solution)/shard_map/pallas_call | solution.py:275
  43.4 1.4 %collective-permute-done.8 = f32[40,1024]{1,0:T(8,128)S(1)} collective-permute-done((f32[40,1024]{1,0:T(8,128)S(1)}, f32[40,1024]{1,0:T(8,128)S(1)}, u32[]{:S(2)}, u32[]{:S(2)}) %collective-permute-start.8) | collective-permute-done | bytes 163872 | tf_op jit(solution)/shard_map/ppermute | solution.py:290
  44.8 2.9 %collective-permute-start.9 = (f32[40,1024]{1,0:T(8,128)S(1)}, f32[40,1024]{1,0:T(8,128)S(1)}, u32[]{:S(2)}, u32[]{:S(2)}) collective-permute-start(f32[40,1024]{1,0:T(8,128)S(1)} %add.11.own_ref), channel_id=1, source_target_pairs={{0,16},{4,20},{8,24},{12,28},{16,0},{20,4},{24,8},{28,12},{1,17},{... | collective-permute-start | bytes 491528 | tf_op jit(solution)/shard_map/ppermute | solution.py:290
  47.7 3.2 %shard_map.72 = (f32[640,1024]{1,0:T(8,128)S(1)}, f32[32,1024]{1,0:T(8,128)S(1)}) custom-call(f32[672,1024]{1,0:T(8,128)S(1)} %get-tuple-element.18.moments_ref, f32[672,1024]{1,0:T(8,128)S(1)} %get-tuple-element.19.more_ref), custom_call_target="tpu_custom_call" | custom-call | flops 4000000000 | bytes 1048576 | tf_op jit(solution)/shard_map/pallas_call | solution.py:275
  50.8 4.3 %collective-permute-done.9.other_ref = f32[40,1024]{1,0:T(8,128)S(1)} collective-permute-done((f32[40,1024]{1,0:T(8,128)S(1)}, f32[40,1024]{1,0:T(8,128)S(1)}, u32[]{:S(2)}, u32[]{:S(2)}) %collective-permute-start.9) | collective-permute-done | bytes 163872 | tf_op jit(solution)/shard_map/ppermute | solution.py:290
  55.2 1.8 %shard_map.73 = (f32[32,1024]{1,0:T(8,128)}, f32[1,1024]{1,0:T(1,128)}) custom-call(f32[640,1024]{1,0:T(8,128)S(1)} %get-tuple-element.20.lower_ref, f32[32,1024]{1,0:T(8,128)S(1)} %get-tuple-element.21.scale_ref, f32[672,1024]{1,0:T(8,128)S(1)} %get-tuple-element.18.moments_ref, f32[672,1024]{1,0:T(8,128)S(1)} %get-tuple-element.19.more_ref, ...), custom_call_target="tpu_custom_call" | custom-call | flops 1000000000 | bytes 1048576 | tf_op jit(solution)/shard_map/pallas_call | solution.py:275
  (25 shorter events, 1.1 us)
Async XLA Ops:
  0.6 18.1 %copy-start.7 = (s32[256]{0:T(256)S(1)}, s32[256]{0:T(256)}, u32[]{:S(2)}) copy-start(s32[256]{0:T(256)} %param.5) | copy-start | bytes 3076
  0.6 0.9 %copy-start = (f32[1024,32]{0,1:T(8,128)S(1)}, f32[1024,32]{0,1:T(8,128)}, u32[]{:S(2)}) copy-start(f32[1024,32]{0,1:T(8,128)} %param.7) | copy-start | bytes 393220
  1.6 1.2 %copy-start.2 = (s32[256,1024]{1,0:T(8,128)S(1)}, s32[256,1024]{1,0:T(8,128)}, u32[]{:S(2)}) copy-start(s32[256,1024]{1,0:T(8,128)} %counts_ref.3) | copy-start | bytes 3145732
  2.8 0.8 %copy-start.4 = (f32[256,32]{0,1:T(8,128)S(1)}, f32[256,32]{0,1:T(8,128)}, u32[]{:S(2)}) copy-start(f32[256,32]{0,1:T(8,128)} %param.6) | copy-start | bytes 98308
  3.5 0.7 %copy-start.6 = (s32[256]{0:T(256)S(1)}, s32[256]{0:T(256)}, u32[]{:S(2)}) copy-start(s32[256]{0:T(256)} %param.5) | copy-start | bytes 3076
  4.2 14.5 %copy-start.5 = (f32[256,32]{0,1:T(8,128)S(1)}, f32[256,32]{0,1:T(8,128)}, u32[]{:S(2)}) copy-start(f32[256,32]{0,1:T(8,128)} %param.6) | copy-start | bytes 98308
  5.5 24.6 %copy-start.1 = (f32[1024,32]{0,1:T(8,128)S(1)}, f32[1024,32]{0,1:T(8,128)}, u32[]{:S(2)}) copy-start(f32[1024,32]{0,1:T(8,128)} %param.7) | copy-start | bytes 393220
  5.5 24.6 %copy-start.3 = (s32[256,1024]{1,0:T(8,128)S(1)}, s32[256,1024]{1,0:T(8,128)}, u32[]{:S(2)}) copy-start(s32[256,1024]{1,0:T(8,128)} %counts_ref.3) | copy-start | bytes 3145732
  5.5 1.8 %collective-permute-start = (f32[672,128]{1,0:T(8,128)S(1)}, f32[672,128]{1,0:T(8,128)S(1)}, u32[]{:S(2)}, u32[]{:S(2)}) collective-permute-start(f32[672,128]{1,0:T(8,128)S(1)} %get-tuple-element.16), channel_id=1, source_target_pairs={{0,1},{1,0},{2,3},{3,2},{4,5},{5,4},{6,7},{7,6},{8,9},{9,8},{10,11... | collective-permute-start | bytes 1032200 | tf_op jit(solution)/shard_map/ppermute | solution.py:290
  7.4 11.3 %collective-permute-start.1 = (f32[672,128]{1,0:T(8,128)S(1)}, f32[672,128]{1,0:T(8,128)S(1)}, u32[]{:S(2)}, u32[]{:S(2)}) collective-permute-start(f32[672,128]{1,0:T(8,128)S(1)} %add.9.own_ref), channel_id=1, source_target_pairs={{0,2},{1,3},{2,0},{3,1},{4,6},{5,7},{6,4},{7,5},{8,10},{9,11},{10,... | collective-permute-start | bytes 1032200 | tf_op jit(solution)/shard_map/ppermute | solution.py:290
  19.6 4.7 %collective-permute-start.3 = (f32[1,40,128]{2,1,0:T(8,128)S(1)}, f32[1,40,128]{2,1,0:T(8,128)S(1)}, u32[]{:S(2)}, u32[]{:S(2)}) collective-permute-start(f32[1,40,128]{2,1,0:T(8,128)S(1)} %shard_map.68.mine_ref), channel_id=1, source_target_pairs={{0,16},{4,20},{8,24},{12,28},{16,0},{20,4},{24,8},{28,12},{1,17},{... | collective-permute-start | bytes 61448 | tf_op jit(solution)/shard_map/ppermute | solution.py:290
  24.4 4.0 %collective-permute-start.4 = (f32[2,40,128]{2,1,0:T(8,128)S(1)}, f32[2,40,128]{2,1,0:T(8,128)S(1)}, u32[]{:S(2)}, u32[]{:S(2)}) collective-permute-start(f32[2,40,128]{2,1,0:T(8,128)S(1)} %pad_maximum_fusion.2), channel_id=1, source_target_pairs={{0,8},{4,12},{8,0},{12,4},{16,24},{20,28},{24,16},{28,20},{1,9},{5... | collective-permute-start | bytes 122888 | tf_op jit(solution)/shard_map/ppermute | solution.py:290
  26.2 3.9 %collective-permute-start.2 = (f32[1,40,128]{2,1,0:T(8,128)S(1)}, f32[1,40,128]{2,1,0:T(8,128)S(1)}, u32[]{:S(2)}, u32[]{:S(2)}) collective-permute-start(f32[1,40,128]{2,1,0:T(8,128)S(1)} %shard_map.68.mine_ref), channel_id=1, source_target_pairs={{0,1},{1,0},{2,3},{3,2},{4,5},{5,4},{6,7},{7,6},{8,9},{9,8},{10,11... | collective-permute-start | bytes 61448 | tf_op jit(solution)/shard_map/ppermute | solution.py:290
  28.4 5.3 %collective-permute-start.5 = (f32[4,40,128]{2,1,0:T(8,128)S(1)}, f32[4,40,128]{2,1,0:T(8,128)S(1)}, u32[]{:S(2)}, u32[]{:S(2)}) collective-permute-start(f32[4,40,128]{2,1,0:T(8,128)S(1)} %pad_maximum_fusion.1), channel_id=1, source_target_pairs={{0,4},{4,0},{8,12},{12,8},{16,20},{20,16},{24,28},{28,24},{1,5},{5... | collective-permute-start | bytes 245768 | tf_op jit(solution)/shard_map/ppermute | solution.py:290
  31.1 6.9 %collective-permute-start.7 = (f32[40,1024]{1,0:T(8,128)S(1)}, f32[40,1024]{1,0:T(8,128)S(1)}, u32[]{:S(2)}, u32[]{:S(2)}) collective-permute-start(f32[40,1024]{1,0:T(8,128)S(1)} %get-tuple-element.24), channel_id=1, source_target_pairs={{0,4},{4,0},{8,12},{12,8},{16,20},{20,16},{24,28},{28,24},{1,5},{5... | collective-permute-start | bytes 491528 | tf_op jit(solution)/shard_map/ppermute | solution.py:290
  33.7 5.4 %collective-permute-start.6 = (f32[8,40,128]{2,1,0:T(8,128)S(1)}, f32[8,40,128]{2,1,0:T(8,128)S(1)}, u32[]{:S(2)}, u32[]{:S(2)}) collective-permute-start(f32[8,40,128]{2,1,0:T(8,128)S(1)} %pad_maximum_fusion.blocks_ref), channel_id=1, source_target_pairs={{0,1},{1,0},{2,3},{3,2},{4,5},{5,4},{6,7},{7,6},{8,9},{9,8},{10,11... | collective-permute-start | bytes 491528 | tf_op jit(solution)/shard_map/ppermute | solution.py:290
  38.1 6.7 %collective-permute-start.8 = (f32[40,1024]{1,0:T(8,128)S(1)}, f32[40,1024]{1,0:T(8,128)S(1)}, u32[]{:S(2)}, u32[]{:S(2)}) collective-permute-start(f32[40,1024]{1,0:T(8,128)S(1)} %add.10), channel_id=1, source_target_pairs={{0,8},{4,12},{8,0},{12,4},{16,24},{20,28},{24,16},{28,20},{1,9},{5... | collective-permute-start | bytes 491528 | tf_op jit(solution)/shard_map/ppermute | solution.py:290
  44.8 10.4 %collective-permute-start.9 = (f32[40,1024]{1,0:T(8,128)S(1)}, f32[40,1024]{1,0:T(8,128)S(1)}, u32[]{:S(2)}, u32[]{:S(2)}) collective-permute-start(f32[40,1024]{1,0:T(8,128)S(1)} %add.11.own_ref), channel_id=1, source_target_pairs={{0,16},{4,20},{8,24},{12,28},{16,0},{20,4},{24,8},{28,12},{1,17},{... | collective-permute-start | bytes 491528 | tf_op jit(solution)/shard_map/ppermute | solution.py:290
where the time goes:
time: 57.2 us; the launch traced here: 57 us
  waiting for transfers between devices  21.7 us (38%)
  Pallas kernels  16.6 us (29%)
  starting transfers between devices  14.2 us (25%)
  local copies, waits for them, and re-layouts  3.58 us (6%)
  between operations  0.75 us (1%)
    ppermute x10, waiting for transfers between devices, exchange(): return lax.ppermute(x, axis, [(i, i ^ bit) for i in range(size)])  21.7 us
    pallas_call x7, Pallas kernels, call(): pl.pallas_call(body, out_shape=outs, in_specs=[single] * len(args), out_s...  16.6 us
    ppermute x10, starting transfers between devices, exchange(): return lax.ppermute(x, axis, [(i, i ^ bit) for i in range(size)])  14.2 us
    unnamed x16, local copies, waits for them, and re-layouts  3.58 us
  transfers between devices with their start and end apart: 10, of which 7 were waited for; matrix products, arithmetic and copies ran while one was open for 0% of the time, Pallas kernels for 22%

commit v1 on v0

--- a/solution.py
+++ b/solution.py
@@ -13,6 +13,7 @@
 DAMPING = 0.1
 SCALE_TOTAL = 5000.0
 SUB = 8
+LANES = 128
 MIB = 1024 * 1024
 
 
@@ -101,86 +102,109 @@
     return answer
 
 
-def factor_moments_kernel(width, counts_ref, totals_ref, ut_ref, vt_ref, mine_ref, theirs_ref, keep_ref, table_ref):
+def halves(ref):
+    half = ref.shape[1] // 2
+    core = lax.rem(lax.axis_index("gene"), 2)
+    return [ref[:, pl.ds(pl.multiple_of(index * half, half), half)] for index in (core, 1 - core)]
+
+
+def factor_gradient_kernel(counts_hbm, totals_hbm, ut_hbm, vt_hbm, mine_ref, theirs_ref, exact_ref, offset_ref, ut_ref, vt_ref, counts_ref, totals_ref, sems):
+    copies = [
+        pltpu.make_async_copy(source, target, sems.at[k])
+        for k, (source, target) in enumerate(
+            ((totals_hbm, totals_ref), (ut_hbm, ut_ref), (vt_hbm, vt_ref), (counts_hbm, counts_ref))
+        )
+    ]
+    for copy in copies:
+        copy.start()
+    for copy in copies[:3]:
+        copy.wait()
     half = ut_ref.shape[1] // 2
     core = lax.rem(lax.axis_index("gene"), 2)
-    parts = (pl.multiple_of(core * half, half), pl.multiple_of((1 - core) * half, half))
-    offset = jnp.log(totals_ref[...].astype(jnp.float32)) - math.log(SCALE_TOTAL)
-    keep_ref[...] = jnp.zeros_like(keep_ref)
-    keep_ref[0:1] = offset
+    offset_ref[...] = jnp.log(totals_ref[...].astype(jnp.float32)) - math.log(SCALE_TOTAL)
+    vt = vt_ref[...]
+    right = stack_right(vt)
+    low = vt.astype(jnp.bfloat16)
+    linear = [
+        lax.dot_general(stack_left(ut, offset), right, (((0,), (0,)), ((), ())), preferred_element_type=jnp.float32)
+        for ut, offset in zip(halves(ut_ref), halves(offset_ref))
+    ]
+    copies[3].wait()
+    for index, lin, out_ref in ((core, linear[0], mine_ref), (1 - core, linear[1], theirs_ref)):
+        part = pl.ds(pl.multiple_of(index * half, half), half)
+        counts = counts_ref[part, :].astype(jnp.float32)
+        exact_ref[part, :] = counts.astype(jnp.bfloat16)
+        residual = (counts - jnp.exp(lin)).astype(jnp.bfloat16)
+        out_ref[...] = lax.dot_general(low, residual, (((1,), (1,)), ((), ())), preferred_element_type=jnp.float32)
+
+
+def factor_moments_kernel(width, add, *refs):
+    (vt_ref, offset_ref, ut_ref), before, (mine_ref, theirs_ref, table_ref) = refs[:3], refs[3:-3], refs[-3:]
+    half = ut_ref.shape[1] // 2
     vt = vt_ref[...]
     fill_table(table_ref, vt, width)
-    right = stack_right(vt)
-    low = vt.astype(jnp.bfloat16)
-    across = (((1,), (1,)), ((), ()))
-    for part, out_ref in zip(parts, (mine_ref, theirs_ref)):
-        left = stack_left(ut_ref[:, pl.ds(part, half)], keep_ref[0:1, pl.ds(part, half)])
-        linear = lax.dot_general(
-            left, right, (((0,), (0,)), ((), ())), preferred_element_type=jnp.float32
-        )
-        expected = jnp.exp(linear)
-        weights = expected.astype(jnp.bfloat16)
-        counts = counts_ref[pl.ds(part, half), :].astype(jnp.float32)
-        residual = (counts - expected).astype(jnp.bfloat16)
-        rows = table_ref.shape[0]
-        out_ref[:rows] = lax.dot_general(table_ref[...], weights, across, preferred_element_type=jnp.float32)
-        out_ref[rows:] = lax.dot_general(low, residual, across, preferred_element_type=jnp.float32)
-
-
-def factor_solve_kernel(width, own_ref, other_ref, totals_ref, ut_ref, new_ref):
+    left = [stack_left(ut, offset) for ut, offset in zip(halves(ut_ref), halves(offset_ref))]
+    linear = lax.dot_general(
+        stack_right(vt), jnp.concatenate(left, axis=1), (((0,), (0,)), ((), ())), preferred_element_type=jnp.float32
+    )
+    weights = jnp.exp(linear).astype(jnp.bfloat16)
+    product = jnp.dot(table_ref[...], weights, preferred_element_type=jnp.float32)
+    for k, out_ref in enumerate((mine_ref, theirs_ref)):
+        total = product[:, k * half : (k + 1) * half]
+        if add:
+            total = total + before[k][...]
+        out_ref[...] = total
+
+
+def factor_solve_kernel(width, terms, *refs):
+    moments, (own_ref, other_ref, offset_ref, ut_ref, new_ref) = refs[:terms], refs[terms:]
     half = own_ref.shape[1]
-    core = lax.rem(lax.axis_index("gene"), 2)
-    part = pl.multiple_of(core * half, half)
-    pieces = table_pieces(width)
-    place = {piece: SUB * p for p, piece in enumerate(pieces)}
-    base = SUB * len(pieces)
+    place = {piece: SUB * p for p, piece in enumerate(table_pieces(width))}
 
     def get(a, q):
         at = place[a, q]
-        return own_ref[at : at + SUB, :] + other_ref[at : at + SUB, :]
-
-    ut = ut_ref[:, pl.ds(part, half)]
+        return sum(ref[at : at + SUB, :] for ref in moments)
+
+    ut = halves(ut_ref)[0]
     right = []
     for q in range(width // SUB):
-        at = base + SUB * q
-        gradient = own_ref[at : at + SUB, :] + other_ref[at : at + SUB, :]
-        right.append(gradient - RIDGE * ut[SUB * q : SUB * q + SUB])
+        rows = slice(SUB * q, SUB * q + SUB)
+        right.append(own_ref[rows] + other_ref[rows] - RIDGE * ut[rows])
     columns, scales = cholesky_columns(get, lambda a, q, v: None, width, half)
     step = cholesky_substitute(columns, scales, right, width, half)
-    offset = jnp.log(totals_ref[:, pl.ds(part, half)].astype(jnp.float32)) - math.log(SCALE_TOTAL)
     new_ref[...] = jnp.zeros_like(new_ref)
     for q in range(width // SUB):
         new_ref[0, SUB * q : SUB * q + SUB, :] = ut[SUB * q : SUB * q + SUB] + step[q]
-    new_ref[0, width : width + 1, :] = offset
-
-
-def counts_kernel(width, counts_ref, mine_ref, theirs_ref, vt_ref, factors_ref, linear_ref):
+    new_ref[0, width : width + 1, :] = halves(offset_ref)[0]
+
+
+def counts_kernel(width, exact_ref, mine_ref, theirs_ref, vt_ref, factors_ref, linear_ref):
     half = mine_ref.shape[2]
+    genes = exact_ref.shape[1]
     core = lax.rem(lax.axis_index("gene"), 2)
-    total = jnp.zeros((width, counts_ref.shape[1]), jnp.float32)
-    terms = jnp.zeros((1, counts_ref.shape[1]), jnp.float32)
-    for own, block_ref in ((1, mine_ref), (0, theirs_ref)):
-        index = core if own else 1 - core
-        part = pl.multiple_of(index * half, half)
+    total = jnp.zeros((width, genes), jnp.float32)
+    terms = jnp.zeros((1, genes), jnp.float32)
+    for index, block_ref in ((core, mine_ref), (1 - core, theirs_ref)):
+        part = pl.ds(pl.multiple_of(index * half, half), half)
         block = block_ref[0]
         factors = block[:width]
-        factors_ref[:, pl.ds(part, half)] = factors
-        counts = counts_ref[pl.ds(part, half), :].astype(jnp.float32)
-        exact = counts.astype(jnp.bfloat16)
+        factors_ref[:, part] = factors
+        exact = exact_ref[part, :]
         high, mid, low = three(factors)
-        both = jnp.concatenate([high, mid, low], axis=0)
+        both = jnp.concatenate([high, mid, low, pad_rows(list(three(block[width : width + 1])))], axis=0)
         product = jnp.dot(both, exact, preferred_element_type=jnp.float32)
         total = total + product[:width]
-        full = product[:width] + (product[width : 2 * width] + product[2 * width :])
+        full = product[:width] + (product[width : 2 * width] + product[2 * width : 3 * width])
         terms = terms - jnp.sum(full * vt_ref[...], axis=0, keepdims=True)
-        oh, om, ol = three(block[width : width + 1])
-        offsets = jnp.dot(pad_rows([oh, om, ol]), exact, preferred_element_type=jnp.float32)
+        terms = terms - jnp.sum(product[3 * width : 3 * width + SUB], axis=0, keepdims=True)
+        counts = exact.astype(jnp.float32)
         own_terms = counts * (jnp.log(jnp.maximum(counts, 1.0)) - 1.0)
         terms = terms + jnp.sum(own_terms, axis=0, keepdims=True)
-        terms = terms - jnp.sum(offsets[:SUB], axis=0, keepdims=True)
-    linear_ref[:width] = total
-    linear_ref[width:] = jnp.zeros_like(linear_ref[width:])
-    linear_ref[width : width + 1] = terms
+    groups = genes // LANES
+    for j in range(groups):
+        cols = slice(j * LANES, (j + 1) * LANES)
+        linear_ref[width * j : width * (j + 1), :] = total[:, cols]
+        linear_ref[width * groups + j : width * groups + j + 1, :] = terms[:, cols]
 
 
 def loading_moments_kernel(width, per, tile, blocks_ref, vt_ref, out_ref, sum_ref, table_ref, left_ref, right_ref):
@@ -246,15 +270,22 @@
     base = SUB * len(place)
     blocks = width // SUB
 
-    @pl.loop(0, genes // tile)
-    def _(j):
-        at = pl.ds(pl.multiple_of(j * tile, tile), tile)
+    groups = genes // LANES
+
+    def seen(first, count):
+        parts = [own_ref[f : f + count] + other_ref[f : f + count] for f in first]
+        return jnp.concatenate(parts, axis=1)
+
+    for j in range(genes // tile):
+        at = slice(j * tile, (j + 1) * tile)
+        lanes = range(j * tile // LANES, (j + 1) * tile // LANES)
         right = []
         for q in range(blocks):
             rows = slice(SUB * q, SUB * q + SUB)
             expected = moments_ref[base + SUB * q : base + SUB * q + SUB, at]
             expected = expected + more_ref[base + SUB * q : base + SUB * q + SUB, at]
-            right.append(own_ref[rows, at] + other_ref[rows, at] - expected - RIDGE * vt_ref[rows, at])
+            counted = seen([width * g + SUB * q for g in lanes], SUB)
+            right.append(counted - expected - RIDGE * vt_ref[rows, at])
         columns = [
             {q: lower_ref[place[k, q] : place[k, q] + SUB, at] for q in range(k // SUB, blocks)} for k in range(width)
         ]
@@ -263,19 +294,20 @@
         for q in range(blocks):
             rows = slice(SUB * q, SUB * q + SUB)
             new_ref[rows, at] = vt_ref[rows, at] + step[q]
-        last = slice(width, width + 1)
-        fixed = own_ref[last, at] + other_ref[last, at] + sum_ref[0:1, at] + sums_ref[0:1, at]
+        fixed = seen([width * groups + g for g in lanes], 1) + sum_ref[0:1, at] + sums_ref[0:1, at]
         deviance_ref[:, at] = fixed * (2.0 / total_cells)
 
 
-def kernel_call(body, outs, scratch, flops, limit=8):
+def kernel_call(body, outs, scratch, flops, limit=8, space=pltpu.VMEM):
     single = pl.BlockSpec(memory_space=pltpu.VMEM)
 
     def call(*args):
+        if space == pltpu.HBM:
+            args = [pltpu.with_memory_space_constraint(x, pltpu.HBM) for x in args]
         return pl.pallas_call(
             body,
             out_shape=outs,
-            in_specs=[single] * len(args),
+            in_specs=[pl.BlockSpec(memory_space=space)] * len(args),
             out_specs=jax.tree.map(lambda _: single, outs),
             scratch_shapes=scratch,
             compiler_params=pltpu.CompilerParams(vmem_limit_bytes=limit * MIB),
@@ -300,20 +332,42 @@
     ut, vt = cell_factors.T, gene_loadings.T
     totals = totals.reshape(1, cells)
 
-    mine, theirs = kernel_call(
-        functools.partial(factor_moments_kernel, width),
-        (shape((rows + width, half)), shape((rows + width, half))),
-        [pltpu.VMEM((SUB, cells), jnp.float32), pltpu.VMEM((rows, genes), jnp.bfloat16)],
+    gene_bits = [1 << k for k in range(1, (lax.axis_size("gene") - 1).bit_length())]
+    across = [vt]
+    for bit in gene_bits:
+        across = across + [exchange(x, "gene", bit) for x in across]
+
+    mine, theirs, exact, offset, ut, vt = kernel_call(
+        factor_gradient_kernel,
+        (
+            shape((width, half)),
+            shape((width, half)),
+            jax.ShapeDtypeStruct((cells, genes), jnp.bfloat16),
+            shape((1, cells)),
+            shape((width, cells)),
+            shape((width, genes)),
+        ),
+        [pltpu.VMEM((cells, genes), jnp.int32), pltpu.VMEM((1, cells), jnp.int32), pltpu.SemaphoreType.DMA((4,))],
         10**9,
+        space=pltpu.HBM,
     )(counts, totals, ut, vt)
     mine = mine + exchange(theirs, "gene", 1)
-    bits = [1 << k for k in range(1, (lax.axis_size("gene") - 1).bit_length())]
-    for bit in bits[:-1]:
+    for bit in gene_bits[:-1]:
         mine = mine + exchange(mine, "gene", bit)
-    other = exchange(mine, "gene", bits[-1])
+    other = exchange(mine, "gene", gene_bits[-1])
+
+    moments = ()
+    for k, x in enumerate([vt] + across[1:]):
+        moments = kernel_call(
+            functools.partial(factor_moments_kernel, width, k > 0),
+            (shape((rows, half)), shape((rows, half))),
+            [pltpu.VMEM((rows, genes), jnp.bfloat16)],
+            10**9,
+        )(x, offset, ut, *moments)
+    moments = (moments[0], exchange(moments[1], "gene", 1))
     block = kernel_call(
-        functools.partial(factor_solve_kernel, width), shape((1, tall, half)), [], 10**9
-    )(mine, other, totals, ut)
+        functools.partial(factor_solve_kernel, width, len(moments)), shape((1, tall, half)), [], 10**9
+    )(*moments, mine, other, offset, ut)
 
     cell_bits = [1 << k for k in range((lax.axis_size("cell") - 1).bit_length())]
     gathered = block
@@ -323,8 +377,8 @@
     opposite = exchange(gathered, "gene", 1)
 
     factors, linear = kernel_call(
-        functools.partial(counts_kernel, width), (shape((width, cells)), shape((tall, genes))), [], 10**9
-    )(counts, block, partner, vt)
+        functools.partial(counts_kernel, width), (shape((width, cells)), shape(((width + 1) * genes // LANES, LANES))), [], 10**9
+    )(exact, block, partner, vt)
     for bit in cell_bits[:-1]:
         linear = linear + exchange(linear, "cell", bit)
     linear_other = exchange(linear, "cell", cell_bits[-1])

time: 57.2 us -> 49.3 us (0.86)
  waiting for transfers between devices: 21.7 us -> 12.9 us
  local copies, waits for them, and re-layouts: 3.58 us -> 0 us
  starting transfers between devices: 14.2 us -> 16.5 us
  Pallas kernels: 16.6 us -> 18.9 us
    ppermute x10 -> x12, waiting for transfers between devices: 21.7 us -> 12.9 us  [exchange(): return lax.ppermute(x, axis, [(i, i ^ bit) for i in range(size)])]
    unnamed x16 -> x0, local copies, waits for them, and re-layouts: 3.58 us -> none
    ppermute x10 -> x12, starting transfers between devices: 14.2 us -> 16.5 us  [exchange(): return lax.ppermute(x, axis, [(i, i ^ bit) for i in range(size)])]
    pallas_call x7 -> x9, Pallas kernels: 16.6 us -> 18.9 us  [call(): pl.pallas_call(body, out_shape=outs, in_specs=[pl.BlockSpec(memory_space=...]
  transfers between devices with their start and end apart: 10 -> 12, of which waited for: 7 -> 7; matrix products, arithmetic and copies ran while one was open for 0% -> 0% of each run, Pallas kernels for 22% -> 31%
where the time goes in v1:
time: 49.3 us; the launch traced here: 49.2 us
  Pallas kernels  18.9 us (38%)
  starting transfers between devices  16.5 us (33%)
  waiting for transfers between devices  12.9 us (26%)
  between operations  0.73 us (1%)
    pallas_call x9, Pallas kernels, call(): pl.pallas_call(body, out_shape=outs, in_specs=[pl.BlockSpec(memory_space=...  18.9 us
    ppermute x12, starting transfers between devices, exchange(): return lax.ppermute(x, axis, [(i, i ^ bit) for i in range(size)])  16.5 us
    ppermute x12, waiting for transfers between devices, exchange(): return lax.ppermute(x, axis, [(i, i ^ bit) for i in range(size)])  12.9 us
  transfers between devices with their start and end apart: 12, of which 7 were waited for; matrix products, arithmetic and copies ran while one was open for 0% of the time, Pallas kernels for 31%

profile of v1, /device:TPU:0, one launch (start us, length us, event | category | flops | bytes accessed | tf_op | source)
XLA Modules:
  0.0 49.2 jit_solution(4622352827144173849)
XLA Ops:
  0.6 3.1 %collective-permute-start = (f32[32,1024]{1,0:T(8,128)}, f32[32,1024]{1,0:T(8,128)S(1)}, u32[]{:S(2)}, u32[]{:S(2)}) collective-permute-start(f32[32,1024]{1,0:T(8,128)} %bitcast.6), channel_id=1, source_target_pairs={{0,2},{1,3},{2,0},{3,1},{4,6},{5,7},{6,4},{7,5},{8,10},{9,11},{10,... | collective-permute-start | bytes 393224 | tf_op jit(solution)/shard_map/ppermute | solution.py:322
  3.7 1.7 %shard_map.67 = (f32[32,128]{1,0:T(8,128)S(1)}, f32[32,128]{1,0:T(8,128)S(1)}, bf16[256,1024]{1,0:T(8,128)(2,1)S(1)}, f32[1,256]{1,0:T(1,128)S(1)}, f32[32,256]{1,0:T(8,128)S(1)}, /*index=5*/f32[32,1024]{1,0:T(8,128)S(1)}) custom-call(s32[256,1024]{1,0:T(8,128)} %counts_hbm.1, s32[1,256]{1,0:T(1,128)} %bitcast.11, f32[32,256]{1,0:T(8,128)} %bitcast.9, ...), custom_call_target="tpu_custom_call" | custom-call | flops 1000000000 | bytes 1048576 | tf_op jit(solution)/shard_map/pallas_call | solution.py:307
  5.4 0.9 %shard_map.68 = (f32[640,128]{1,0:T(8,128)S(1)}, f32[640,128]{1,0:T(8,128)S(1)}) custom-call(f32[32,1024]{1,0:T(8,128)S(1)} %get-tuple-element.26.refs_0_.vt_ref, f32[1,256]{1,0:T(1,128)S(1)} %get-tuple-element.24.refs_1_.refs_4_, f32[32,256]{1,0:T(8,128)S(1)} %get-tuple-element.25.refs_2_.refs_5_), custom_call_target="tpu_custom_call" | custom-call | flops 1000000000 | bytes 1048576 | tf_op jit(solution)/shard_map/pallas_call | solution.py:307
  6.3 1.1 %collective-permute-done.refs_0_ = f32[32,1024]{1,0:T(8,128)S(1)} collective-permute-done((f32[32,1024]{1,0:T(8,128)}, f32[32,1024]{1,0:T(8,128)S(1)}, u32[]{:S(2)}, u32[]{:S(2)}) %collective-permute-start) | collective-permute-done | bytes 131104 | tf_op jit(solution)/shard_map/ppermute | solution.py:322
  7.4 0.9 %shard_map.69 = (f32[640,128]{1,0:T(8,128)S(1)}, f32[640,128]{1,0:T(8,128)S(1)}) custom-call(f32[32,1024]{1,0:T(8,128)S(1)} %collective-permute-done.refs_0_, f32[1,256]{1,0:T(1,128)S(1)} %get-tuple-element.24.refs_1_.refs_4_, f32[32,256]{1,0:T(8,128)S(1)} %get-tuple-element.25.refs_2_.refs_5_, f32[640,128]{1,0:T(8,128)S(1)} %get-tuple-element.27.refs_3_, ...), custom_call_target="tpu_custom_call" | custom-call | flops 1000000000 | bytes 1048576 | tf_op jit(solution)/shard_map/pallas_call | solution.py:307
  8.4 0.5 %collective-permute-start.2 = (f32[32,128]{1,0:T(8,128)S(1)}, f32[32,128]{1,0:T(8,128)S(1)}, u32[]{:S(2)}, u32[]{:S(2)}) collective-permute-start(f32[32,128]{1,0:T(8,128)S(1)} %get-tuple-element.32), channel_id=1, source_target_pairs={{0,1},{1,0},{2,3},{3,2},{4,5},{5,4},{6,7},{7,6},{8,9},{9,8},{10,11... | collective-permute-start | bytes 49160 | tf_op jit(solution)/shard_map/ppermute | solution.py:322
  8.9 1.1 %collective-permute-done.2 = f32[32,128]{1,0:T(8,128)S(1)} collective-permute-done((f32[32,128]{1,0:T(8,128)S(1)}, f32[32,128]{1,0:T(8,128)S(1)}, u32[]{:S(2)}, u32[]{:S(2)}) %collective-permute-start.2) | collective-permute-done | bytes 16416 | tf_op jit(solution)/shard_map/ppermute | solution.py:322
  10.1 1.7 %collective-permute-start.3 = (f32[32,128]{1,0:T(8,128)S(1)}, f32[32,128]{1,0:T(8,128)S(1)}, u32[]{:S(2)}, u32[]{:S(2)}) collective-permute-start(f32[32,128]{1,0:T(8,128)S(1)} %add.9.refs_2_), channel_id=1, source_target_pairs={{0,2},{1,3},{2,0},{3,1},{4,6},{5,7},{6,4},{7,5},{8,10},{9,11},{10,... | collective-permute-start | bytes 49160 | tf_op jit(solution)/shard_map/ppermute | solution.py:322
  11.8 2.0 %collective-permute-done.3.refs_3_ = f32[32,128]{1,0:T(8,128)S(1)} collective-permute-done((f32[32,128]{1,0:T(8,128)S(1)}, f32[32,128]{1,0:T(8,128)S(1)}, u32[]{:S(2)}, u32[]{:S(2)}) %collective-permute-start.3) | collective-permute-done | bytes 16416 | tf_op jit(solution)/shard_map/ppermute | solution.py:322
  13.8 0.9 %shard_map.70.mine_ref = f32[1,40,128]{2,1,0:T(8,128)S(1)} custom-call(f32[640,128]{1,0:T(8,128)S(1)} %get-tuple-element.29.refs_0_, f32[640,128]{1,0:T(8,128)S(1)} %collective-permute-done.1.refs_1_, f32[32,128]{1,0:T(8,128)S(1)} %add.9.refs_2_, f32[32,128]{1,0:T(8,128)S(1)} %collective-permute-done.3.refs_3_, ...), custom_call_target="tpu_custom_call" | custom-call | flops 1000000000 | bytes 1048576 | tf_op jit(solution)/shard_map/pallas_call | solution.py:307
  14.7 2.9 %collective-permute-start.5 = (f32[1,40,128]{2,1,0:T(8,128)S(1)}, f32[1,40,128]{2,1,0:T(8,128)S(1)}, u32[]{:S(2)}, u32[]{:S(2)}) collective-permute-start(f32[1,40,128]{2,1,0:T(8,128)S(1)} %shard_map.70.mine_ref), channel_id=1, source_target_pairs={{0,16},{4,20},{8,24},{12,28},{16,0},{20,4},{24,8},{28,12},{1,17},{... | collective-permute-start | bytes 61448 | tf_op jit(solution)/shard_map/ppermute | solution.py:322
  17.6 1.9 %collective-permute-done.5 = f32[1,40,128]{2,1,0:T(8,128)S(1)} collective-permute-done((f32[1,40,128]{2,1,0:T(8,128)S(1)}, f32[1,40,128]{2,1,0:T(8,128)S(1)}, u32[]{:S(2)}, u32[]{:S(2)}) %collective-permute-start.5) | collective-permute-done | bytes 20512 | tf_op jit(solution)/shard_map/ppermute | solution.py:322
  19.5 1.8 %collective-permute-start.6 = (f32[2,40,128]{2,1,0:T(8,128)S(1)}, f32[2,40,128]{2,1,0:T(8,128)S(1)}, u32[]{:S(2)}, u32[]{:S(2)}) collective-permute-start(f32[2,40,128]{2,1,0:T(8,128)S(1)} %pad_maximum_fusion.2), channel_id=1, source_target_pairs={{0,8},{4,12},{8,0},{12,4},{16,24},{20,28},{24,16},{28,20},{1,9},{5... | collective-permute-start | bytes 122888 | tf_op jit(solution)/shard_map/ppermute | solution.py:322
  21.3 2.2 %collective-permute-done.6 = f32[2,40,128]{2,1,0:T(8,128)S(1)} collective-permute-done((f32[2,40,128]{2,1,0:T(8,128)S(1)}, f32[2,40,128]{2,1,0:T(8,128)S(1)}, u32[]{:S(2)}, u32[]{:S(2)}) %collective-permute-start.6) | collective-permute-done | bytes 40992 | tf_op jit(solution)/shard_map/ppermute | solution.py:322
  23.5 1.7 %collective-permute-start.7 = (f32[4,40,128]{2,1,0:T(8,128)S(1)}, f32[4,40,128]{2,1,0:T(8,128)S(1)}, u32[]{:S(2)}, u32[]{:S(2)}) collective-permute-start(f32[4,40,128]{2,1,0:T(8,128)S(1)} %pad_maximum_fusion.1), channel_id=1, source_target_pairs={{0,4},{4,0},{8,12},{12,8},{16,20},{20,16},{24,28},{28,24},{1,5},{5... | collective-permute-start | bytes 245768 | tf_op jit(solution)/shard_map/ppermute | solution.py:322
  25.2 1.0 %shard_map.71 = (f32[32,256]{1,0:T(8,128)}, f32[264,128]{1,0:T(8,128)S(1)}) custom-call(bf16[256,1024]{1,0:T(8,128)(2,1)S(1)} %get-tuple-element.23.exact_ref, f32[1,40,128]{2,1,0:T(8,128)S(1)} %shard_map.70.mine_ref, f32[1,40,128]{2,1,0:T(8,128)S(1)} %collective-permute-done.4.theirs_ref, f32[32,1024]{1,0:T(8,128)S(1)} %get-tuple-element.26.refs_0_.vt_ref), custom_call_target="tpu_custom_call" | custom-call | flops 1000000000 | bytes 1048576 | tf_op jit(solution)/shard_map/pallas_call | solution.py:307
  26.5 2.3 %collective-permute-done.7 = f32[4,40,128]{2,1,0:T(8,128)S(1)} collective-permute-done((f32[4,40,128]{2,1,0:T(8,128)S(1)}, f32[4,40,128]{2,1,0:T(8,128)S(1)}, u32[]{:S(2)}, u32[]{:S(2)}) %collective-permute-start.7) | collective-permute-done | bytes 81952 | tf_op jit(solution)/shard_map/ppermute | solution.py:322
  28.9 2.3 %collective-permute-done.9 = f32[264,128]{1,0:T(8,128)S(1)} collective-permute-done((f32[264,128]{1,0:T(8,128)S(1)}, f32[264,128]{1,0:T(8,128)S(1)}, u32[]{:S(2)}, u32[]{:S(2)}) %collective-permute-start.9) | collective-permute-done | bytes 135200 | tf_op jit(solution)/shard_map/ppermute | solution.py:322
  31.2 1.6 %collective-permute-start.10 = (f32[264,128]{1,0:T(8,128)S(1)}, f32[264,128]{1,0:T(8,128)S(1)}, u32[]{:S(2)}, u32[]{:S(2)}) collective-permute-start(f32[264,128]{1,0:T(8,128)S(1)} %add.10), channel_id=1, source_target_pairs={{0,8},{4,12},{8,0},{12,4},{16,24},{20,28},{24,16},{28,20},{1,9},{5... | collective-permute-start | bytes 405512 | tf_op jit(solution)/shard_map/ppermute | solution.py:322
  32.8 4.2 %shard_map.72 = (f32[672,1024]{1,0:T(8,128)S(1)}, f32[8,1024]{1,0:T(8,128)S(1)}) custom-call(f32[8,40,128]{2,1,0:T(8,128)S(1)} %pad_maximum_fusion.blocks_ref, f32[32,1024]{1,0:T(8,128)S(1)} %get-tuple-element.26.refs_0_.vt_ref), custom_call_target="tpu_custom_call" | custom-call | flops 4000000000 | bytes 1048576 | tf_op jit(solution)/shard_map/pallas_call | solution.py:307
  37.1 2.8 %collective-permute-start.11 = (f32[264,128]{1,0:T(8,128)S(1)}, f32[264,128]{1,0:T(8,128)S(1)}, u32[]{:S(2)}, u32[]{:S(2)}) collective-permute-start(f32[264,128]{1,0:T(8,128)S(1)} %add.11.own_ref), channel_id=1, source_target_pairs={{0,16},{4,20},{8,24},{12,28},{16,0},{20,4},{24,8},{28,12},{1,17},{... | collective-permute-start | bytes 405512 | tf_op jit(solution)/shard_map/ppermute | solution.py:322
  39.9 4.2 %shard_map.73 = (f32[672,1024]{1,0:T(8,128)S(1)}, f32[8,1024]{1,0:T(8,128)S(1)}) custom-call(f32[8,40,128]{2,1,0:T(8,128)S(1)} %collective-permute-done.8.blocks_ref, f32[32,1024]{1,0:T(8,128)S(1)} %get-tuple-element.26.refs_0_.vt_ref), custom_call_target="tpu_custom_call" | custom-call | flops 4000000000 | bytes 1048576 | tf_op jit(solution)/shard_map/pallas_call | solution.py:307
  44.1 3.2 %shard_map.74 = (f32[640,1024]{1,0:T(8,128)S(1)}, f32[32,1024]{1,0:T(8,128)S(1)}) custom-call(f32[672,1024]{1,0:T(8,128)S(1)} %get-tuple-element.34.moments_ref, f32[672,1024]{1,0:T(8,128)S(1)} %get-tuple-element.35.more_ref), custom_call_target="tpu_custom_call" | custom-call | flops 4000000000 | bytes 1048576 | tf_op jit(solution)/shard_map/pallas_call | solution.py:307
  47.3 1.9 %shard_map.75 = (f32[32,1024]{1,0:T(8,128)}, f32[1,1024]{1,0:T(1,128)}) custom-call(f32[640,1024]{1,0:T(8,128)S(1)} %get-tuple-element.36.lower_ref, f32[32,1024]{1,0:T(8,128)S(1)} %get-tuple-element.37.scale_ref, f32[672,1024]{1,0:T(8,128)S(1)} %get-tuple-element.34.moments_ref, f32[672,1024]{1,0:T(8,128)S(1)} %get-tuple-element.35.more_ref, ...), custom_call_target="tpu_custom_call" | custom-call | flops 1000000000 | bytes 1048576 | tf_op jit(solution)/shard_map/pallas_call | solution.py:307
  (15 shorter events, 0.5 us)
Async XLA Ops:
  0.6 6.8 %collective-permute-start = (f32[32,1024]{1,0:T(8,128)}, f32[32,1024]{1,0:T(8,128)S(1)}, u32[]{:S(2)}, u32[]{:S(2)}) collective-permute-start(f32[32,1024]{1,0:T(8,128)} %bitcast.6), channel_id=1, source_target_pairs={{0,2},{1,3},{2,0},{3,1},{4,6},{5,7},{6,4},{7,5},{8,10},{9,11},{10,... | collective-permute-start | bytes 393224 | tf_op jit(solution)/shard_map/ppermute | solution.py:322
  8.3 5.5 %collective-permute-start.1 = (f32[640,128]{1,0:T(8,128)S(1)}, f32[640,128]{1,0:T(8,128)S(1)}, u32[]{:S(2)}, u32[]{:S(2)}) collective-permute-start(f32[640,128]{1,0:T(8,128)S(1)} %get-tuple-element.30), channel_id=1, source_target_pairs={{0,1},{1,0},{2,3},{3,2},{4,5},{5,4},{6,7},{7,6},{8,9},{9,8},{10,11... | collective-permute-start | bytes 983048 | tf_op jit(solution)/shard_map/ppermute | solution.py:322
  8.4 1.6 %collective-permute-start.2 = (f32[32,128]{1,0:T(8,128)S(1)}, f32[32,128]{1,0:T(8,128)S(1)}, u32[]{:S(2)}, u32[]{:S(2)}) collective-permute-start(f32[32,128]{1,0:T(8,128)S(1)} %get-tuple-element.32), channel_id=1, source_target_pairs={{0,1},{1,0},{2,3},{3,2},{4,5},{5,4},{6,7},{7,6},{8,9},{9,8},{10,11... | collective-permute-start | bytes 49160 | tf_op jit(solution)/shard_map/ppermute | solution.py:322
  10.1 3.7 %collective-permute-start.3 = (f32[32,128]{1,0:T(8,128)S(1)}, f32[32,128]{1,0:T(8,128)S(1)}, u32[]{:S(2)}, u32[]{:S(2)}) collective-permute-start(f32[32,128]{1,0:T(8,128)S(1)} %add.9.refs_2_), channel_id=1, source_target_pairs={{0,2},{1,3},{2,0},{3,1},{4,6},{5,7},{6,4},{7,5},{8,10},{9,11},{10,... | collective-permute-start | bytes 49160 | tf_op jit(solution)/shard_map/ppermute | solution.py:322
  14.7 4.7 %collective-permute-start.5 = (f32[1,40,128]{2,1,0:T(8,128)S(1)}, f32[1,40,128]{2,1,0:T(8,128)S(1)}, u32[]{:S(2)}, u32[]{:S(2)}) collective-permute-start(f32[1,40,128]{2,1,0:T(8,128)S(1)} %shard_map.70.mine_ref), channel_id=1, source_target_pairs={{0,16},{4,20},{8,24},{12,28},{16,0},{20,4},{24,8},{28,12},{1,17},{... | collective-permute-start | bytes 61448 | tf_op jit(solution)/shard_map/ppermute | solution.py:322
  19.5 4.0 %collective-permute-start.6 = (f32[2,40,128]{2,1,0:T(8,128)S(1)}, f32[2,40,128]{2,1,0:T(8,128)S(1)}, u32[]{:S(2)}, u32[]{:S(2)}) collective-permute-start(f32[2,40,128]{2,1,0:T(8,128)S(1)} %pad_maximum_fusion.2), channel_id=1, source_target_pairs={{0,8},{4,12},{8,0},{12,4},{16,24},{20,28},{24,16},{28,20},{1,9},{5... | collective-permute-start | bytes 122888 | tf_op jit(solution)/shard_map/ppermute | solution.py:322
  21.3 3.9 %collective-permute-start.4 = (f32[1,40,128]{2,1,0:T(8,128)S(1)}, f32[1,40,128]{2,1,0:T(8,128)S(1)}, u32[]{:S(2)}, u32[]{:S(2)}) collective-permute-start(f32[1,40,128]{2,1,0:T(8,128)S(1)} %shard_map.70.mine_ref), channel_id=1, source_target_pairs={{0,1},{1,0},{2,3},{3,2},{4,5},{5,4},{6,7},{7,6},{8,9},{9,8},{10,11... | collective-permute-start | bytes 61448 | tf_op jit(solution)/shard_map/ppermute | solution.py:322
  23.5 5.3 %collective-permute-start.7 = (f32[4,40,128]{2,1,0:T(8,128)S(1)}, f32[4,40,128]{2,1,0:T(8,128)S(1)}, u32[]{:S(2)}, u32[]{:S(2)}) collective-permute-start(f32[4,40,128]{2,1,0:T(8,128)S(1)} %pad_maximum_fusion.1), channel_id=1, source_target_pairs={{0,4},{4,0},{8,12},{12,8},{16,20},{20,16},{24,28},{28,24},{1,5},{5... | collective-permute-start | bytes 245768 | tf_op jit(solution)/shard_map/ppermute | solution.py:322
  26.2 5.0 %collective-permute-start.9 = (f32[264,128]{1,0:T(8,128)S(1)}, f32[264,128]{1,0:T(8,128)S(1)}, u32[]{:S(2)}, u32[]{:S(2)}) collective-permute-start(f32[264,128]{1,0:T(8,128)S(1)} %get-tuple-element.40), channel_id=1, source_target_pairs={{0,4},{4,0},{8,12},{12,8},{16,20},{20,16},{24,28},{28,24},{1,5},{5... | collective-permute-start | bytes 405512 | tf_op jit(solution)/shard_map/ppermute | solution.py:322
  28.8 11.1 %collective-permute-start.8 = (f32[8,40,128]{2,1,0:T(8,128)S(1)}, f32[8,40,128]{2,1,0:T(8,128)S(1)}, u32[]{:S(2)}, u32[]{:S(2)}) collective-permute-start(f32[8,40,128]{2,1,0:T(8,128)S(1)} %pad_maximum_fusion.blocks_ref), channel_id=1, source_target_pairs={{0,1},{1,0},{2,3},{3,2},{4,5},{5,4},{6,7},{7,6},{8,9},{9,8},{10,11... | collective-permute-start | bytes 491528 | tf_op jit(solution)/shard_map/ppermute | solution.py:322
  31.2 5.9 %collective-permute-start.10 = (f32[264,128]{1,0:T(8,128)S(1)}, f32[264,128]{1,0:T(8,128)S(1)}, u32[]{:S(2)}, u32[]{:S(2)}) collective-permute-start(f32[264,128]{1,0:T(8,128)S(1)} %add.10), channel_id=1, source_target_pairs={{0,8},{4,12},{8,0},{12,4},{16,24},{20,28},{24,16},{28,20},{1,9},{5... | collective-permute-start | bytes 405512 | tf_op jit(solution)/shard_map/ppermute | solution.py:322
  37.1 10.2 %collective-permute-start.11 = (f32[264,128]{1,0:T(8,128)S(1)}, f32[264,128]{1,0:T(8,128)S(1)}, u32[]{:S(2)}, u32[]{:S(2)}) collective-permute-start(f32[264,128]{1,0:T(8,128)S(1)} %add.11.own_ref), channel_id=1, source_target_pairs={{0,16},{4,20},{8,24},{12,28},{16,0},{20,4},{24,8},{28,12},{1,17},{... | collective-permute-start | bytes 405512 | tf_op jit(solution)/shard_map/ppermute | solution.py:322

commit v2 on v1

--- a/solution.py
+++ b/solution.py
@@ -178,7 +178,16 @@
     new_ref[0, width : width + 1, :] = halves(offset_ref)[0]
 
 
-def counts_kernel(width, exact_ref, mine_ref, theirs_ref, vt_ref, factors_ref, linear_ref):
+def pack(out_ref, square, row, first):
+    width = square.shape[0]
+    groups = out_ref.shape[0] // (width + 1)
+    for j in range(groups):
+        cols = slice(first + j * LANES, first + (j + 1) * LANES)
+        out_ref[width * j : width * (j + 1), :] = square[:, cols]
+        out_ref[width * groups + j : width * groups + j + 1, :] = row[:, cols]
+
+
+def counts_kernel(width, exact_ref, mine_ref, theirs_ref, vt_ref, factors_ref, own_ref, other_ref, share_ref):
     half = mine_ref.shape[2]
     genes = exact_ref.shape[1]
     core = lax.rem(lax.axis_index("gene"), 2)
@@ -200,11 +209,15 @@
         counts = exact.astype(jnp.float32)
         own_terms = counts * (jnp.log(jnp.maximum(counts, 1.0)) - 1.0)
         terms = terms + jnp.sum(own_terms, axis=0, keepdims=True)
-    groups = genes // LANES
-    for j in range(groups):
-        cols = slice(j * LANES, (j + 1) * LANES)
-        linear_ref[width * j : width * (j + 1), :] = total[:, cols]
-        linear_ref[width * groups + j : width * groups + j + 1, :] = terms[:, cols]
+    share = genes // 2
+    turn = lax.rem(lax.axis_index("cell"), 2)
+    share_ref[...] = vt_ref[:, pl.ds(pl.multiple_of(turn * share, share), share)]
+    for k in range(2):
+
+        @pl.when(turn == k)
+        def _():
+            pack(own_ref, total, terms, k * share)
+            pack(other_ref, total, terms, (1 - k) * share)
 
 
 def loading_moments_kernel(width, per, tile, blocks_ref, vt_ref, out_ref, sum_ref, table_ref, left_ref, right_ref):
@@ -264,7 +277,7 @@
             scale_ref[k : k + 1, at] = scales[k]
 
 
-def loading_solve_kernel(width, tile, total_cells, lower_ref, scale_ref, moments_ref, more_ref, sum_ref, sums_ref, own_ref, other_ref, vt_ref, new_ref, deviance_ref):
+def loading_solve_kernel(width, tile, total_cells, lower_ref, scale_ref, moments_ref, more_ref, sum_ref, sums_ref, own_ref, other_ref, vt_ref, result_ref):
     genes = vt_ref.shape[1]
     place = {piece: SUB * p for p, piece in enumerate(table_pieces(width))}
     base = SUB * len(place)
@@ -291,11 +304,26 @@
         ]
         scales = [scale_ref[k : k + 1, at] for k in range(width)]
         step = cholesky_substitute(columns, scales, right, width, tile)
-        for q in range(blocks):
-            rows = slice(SUB * q, SUB * q + SUB)
-            new_ref[rows, at] = vt_ref[rows, at] + step[q]
         fixed = seen([width * groups + g for g in lanes], 1) + sum_ref[0:1, at] + sums_ref[0:1, at]
-        deviance_ref[:, at] = fixed * (2.0 / total_cells)
+        fixed = fixed * (2.0 / total_cells)
+        for g in lanes:
+            cols = slice(g * LANES - j * tile, (g + 1) * LANES - j * tile)
+            for q in range(blocks):
+                rows = slice(SUB * q, SUB * q + SUB)
+                here = slice(width * g + SUB * q, width * g + SUB * q + SUB)
+                result_ref[here, :] = vt_ref[rows, at][:, cols] + step[q][:, cols]
+            result_ref[width * groups + g : width * groups + g + 1, :] = fixed[:, cols]
+
+
+def assemble_kernel(width, own_ref, other_ref, new_ref, deviance_ref):
+    groups = own_ref.shape[0] // (width + 1)
+    share = groups * LANES
+    turn = lax.rem(lax.axis_index("cell"), 2)
+    for first, ref in ((turn, own_ref), (1 - turn, other_ref)):
+        for g in range(groups):
+            at = pl.ds(pl.multiple_of(first * share + g * LANES, LANES), LANES)
+            new_ref[:, at] = ref[width * g : width * (g + 1), :]
+            deviance_ref[:, at] = ref[width * groups + g : width * groups + g + 1, :]
 
 
 def kernel_call(body, outs, scratch, flops, limit=8, space=pltpu.VMEM):
@@ -372,17 +400,23 @@
     cell_bits = [1 << k for k in range((lax.axis_size("cell") - 1).bit_length())]
     gathered = block
     for bit in reversed(cell_bits):
-        gathered = jnp.concatenate([gathered, exchange(gathered, "cell", bit)], axis=0)
+        arrived = exchange(gathered, "cell", bit)
+        gathered = jnp.concatenate([gathered, arrived], axis=0)
     partner = exchange(block, "gene", 1)
     opposite = exchange(gathered, "gene", 1)
 
-    factors, linear = kernel_call(
-        functools.partial(counts_kernel, width), (shape((width, cells)), shape(((width + 1) * genes // LANES, LANES))), [], 10**9
+    share = genes // 2
+    packed = shape(((width + 1) * share // LANES, LANES))
+    factors, linear, theirs, vt = kernel_call(
+        functools.partial(counts_kernel, width),
+        (shape((width, cells)), packed, packed, shape((width, share))),
+        [],
+        10**9,
     )(exact, block, partner, vt)
-    for bit in cell_bits[:-1]:
-        linear = linear + exchange(linear, "cell", bit)
-    linear_other = exchange(linear, "cell", cell_bits[-1])
-
+    arrived = exchange(theirs, "cell", 1)
+    for bit in cell_bits[1:]:
+        linear = linear + arrived
+        arrived = exchange(linear, "cell", bit)
     per = min(gathered.shape[0], 8)
     tile = 256
     depth = 6 * width + 16
@@ -390,11 +424,11 @@
     def moments_of(blocks):
         return kernel_call(
             functools.partial(loading_moments_kernel, width, per, tile),
-            (shape((rows + width, genes)), shape((SUB, genes))),
+            (shape((rows + width, share)), shape((SUB, share))),
             [
                 pltpu.VMEM((rows + width, per * half), jnp.bfloat16),
                 pltpu.VMEM((depth, per * half), jnp.bfloat16),
-                pltpu.VMEM((depth, genes), jnp.bfloat16),
+                pltpu.VMEM((depth, share), jnp.bfloat16),
             ],
             4 * 10**9,
             16,
@@ -404,17 +438,17 @@
     more, more_sums = moments_of(opposite)
     lower, scales = kernel_call(
         functools.partial(loading_factor_kernel, width, 256),
-        (shape((rows, genes)), shape((width, genes))),
+        (shape((rows, share)), shape((width, share))),
         [],
         4 * 10**9,
     )(moments, more)
     total_cells = cells * lax.axis_size("cell")
+    result = kernel_call(
+        functools.partial(loading_solve_kernel, width, min(share, 512), total_cells), packed, [], 10**9
+    )(lower, scales, moments, more, sums, more_sums, linear, arrived, vt)
     new_loadings, deviance = kernel_call(
-        functools.partial(loading_solve_kernel, width, min(genes, 1024), total_cells),
-        (shape((width, genes)), shape((1, genes))),
-        [],
-        10**9,
-    )(lower, scales, moments, more, sums, more_sums, linear, linear_other, vt)
+        functools.partial(assemble_kernel, width), (shape((width, genes)), shape((1, genes))), [], 10**6
+    )(result, exchange(result, "cell", 1))
     return (factors.T, new_loadings.T, deviance.reshape(genes))
 
 

time: 49.3 us -> 47.5 us (0.963)
  Pallas kernels: 18.9 us -> 13.1 us
  waiting for transfers between devices: 12.9 us -> 16.4 us
  starting transfers between devices: 16.5 us -> 17 us
    pallas_call x9 -> x10, Pallas kernels: 18.9 us -> 13.1 us  [call(): pl.pallas_call(body, out_shape=outs, in_specs=[pl.BlockSpec(memory_space=...]
    ppermute x12 -> x13, waiting for transfers between devices: 12.9 us -> 16.4 us  [exchange(): return lax.ppermute(x, axis, [(i, i ^ bit) for i in range(size)])]
    ppermute x12 -> x13, starting transfers between devices: 16.5 us -> 17 us  [exchange(): return lax.ppermute(x, axis, [(i, i ^ bit) for i in range(size)])]
  transfers between devices with their start and end apart: 12 -> 13, of which waited for: 7 -> 9; matrix products, arithmetic and copies ran while one was open for 0% -> 0% of each run, Pallas kernels for 31% -> 21%
where the time goes in v2:
time: 47.5 us; the launch traced here: 47.3 us
  starting transfers between devices  17 us (36%)
  waiting for transfers between devices  16.4 us (35%)
  Pallas kernels  13.1 us (28%)
  between operations  0.72 us (2%)
    ppermute x13, starting transfers between devices, exchange(): return lax.ppermute(x, axis, [(i, i ^ bit) for i in range(size)])  17 us
    ppermute x13, waiting for transfers between devices, exchange(): return lax.ppermute(x, axis, [(i, i ^ bit) for i in range(size)])  16.4 us
    pallas_call x10, Pallas kernels, call(): pl.pallas_call(body, out_shape=outs, in_specs=[pl.BlockSpec(memory_space=...  13.1 us
  transfers between devices with their start and end apart: 13, of which 9 were waited for; matrix products, arithmetic and copies ran while one was open for 0% of the time, Pallas kernels for 21%

profile of v2, /device:TPU:0, one launch (start us, length us, event | category | flops | bytes accessed | tf_op | source)
XLA Modules:
  0.0 47.3 jit_solution(3246008315912318098)
XLA Ops:
  0.6 3.1 %collective-permute-start = (f32[32,1024]{1,0:T(8,128)}, f32[32,1024]{1,0:T(8,128)S(1)}, u32[]{:S(2)}, u32[]{:S(2)}) collective-permute-start(f32[32,1024]{1,0:T(8,128)} %bitcast.6), channel_id=1, source_target_pairs={{0,2},{1,3},{2,0},{3,1},{4,6},{5,7},{6,4},{7,5},{8,10},{9,11},{10,... | collective-permute-start | bytes 393224 | tf_op jit(solution)/shard_map/ppermute | solution.py:350
  3.7 1.7 %shard_map.67 = (f32[32,128]{1,0:T(8,128)S(1)}, f32[32,128]{1,0:T(8,128)S(1)}, bf16[256,1024]{1,0:T(8,128)(2,1)S(1)}, f32[1,256]{1,0:T(1,128)S(1)}, f32[32,256]{1,0:T(8,128)S(1)}, /*index=5*/f32[32,1024]{1,0:T(8,128)S(1)}) custom-call(s32[256,1024]{1,0:T(8,128)} %counts_hbm.1, s32[1,256]{1,0:T(1,128)} %bitcast.11, f32[32,256]{1,0:T(8,128)} %bitcast.9, ...), custom_call_target="tpu_custom_call" | custom-call | flops 1000000000 | bytes 1048576 | tf_op jit(solution)/shard_map/pallas_call | solution.py:335
  5.4 0.9 %shard_map.68 = (f32[640,128]{1,0:T(8,128)S(1)}, f32[640,128]{1,0:T(8,128)S(1)}) custom-call(f32[32,1024]{1,0:T(8,128)S(1)} %get-tuple-element.28.refs_0_.vt_ref, f32[1,256]{1,0:T(1,128)S(1)} %get-tuple-element.26.refs_1_.refs_4_, f32[32,256]{1,0:T(8,128)S(1)} %get-tuple-element.27.refs_2_.refs_5_), custom_call_target="tpu_custom_call" | custom-call | flops 1000000000 | bytes 1048576 | tf_op jit(solution)/shard_map/pallas_call | solution.py:335
  6.3 1.1 %collective-permute-done.refs_0_ = f32[32,1024]{1,0:T(8,128)S(1)} collective-permute-done((f32[32,1024]{1,0:T(8,128)}, f32[32,1024]{1,0:T(8,128)S(1)}, u32[]{:S(2)}, u32[]{:S(2)}) %collective-permute-start) | collective-permute-done | bytes 131104 | tf_op jit(solution)/shard_map/ppermute | solution.py:350
  7.4 0.9 %shard_map.69 = (f32[640,128]{1,0:T(8,128)S(1)}, f32[640,128]{1,0:T(8,128)S(1)}) custom-call(f32[32,1024]{1,0:T(8,128)S(1)} %collective-permute-done.refs_0_, f32[1,256]{1,0:T(1,128)S(1)} %get-tuple-element.26.refs_1_.refs_4_, f32[32,256]{1,0:T(8,128)S(1)} %get-tuple-element.27.refs_2_.refs_5_, f32[640,128]{1,0:T(8,128)S(1)} %get-tuple-element.29.refs_3_, ...), custom_call_target="tpu_custom_call" | custom-call | flops 1000000000 | bytes 1048576 | tf_op jit(solution)/shard_map/pallas_call | solution.py:335
  8.9 1.1 %collective-permute-done.2 = f32[32,128]{1,0:T(8,128)S(1)} collective-permute-done((f32[32,128]{1,0:T(8,128)S(1)}, f32[32,128]{1,0:T(8,128)S(1)}, u32[]{:S(2)}, u32[]{:S(2)}) %collective-permute-start.2) | collective-permute-done | bytes 16416 | tf_op jit(solution)/shard_map/ppermute | solution.py:350
  10.1 1.7 %collective-permute-start.3 = (f32[32,128]{1,0:T(8,128)S(1)}, f32[32,128]{1,0:T(8,128)S(1)}, u32[]{:S(2)}, u32[]{:S(2)}) collective-permute-start(f32[32,128]{1,0:T(8,128)S(1)} %add.9.refs_2_), channel_id=1, source_target_pairs={{0,2},{1,3},{2,0},{3,1},{4,6},{5,7},{6,4},{7,5},{8,10},{9,11},{10,... | collective-permute-start | bytes 49160 | tf_op jit(solution)/shard_map/ppermute | solution.py:350
  11.8 2.0 %collective-permute-done.3.refs_3_ = f32[32,128]{1,0:T(8,128)S(1)} collective-permute-done((f32[32,128]{1,0:T(8,128)S(1)}, f32[32,128]{1,0:T(8,128)S(1)}, u32[]{:S(2)}, u32[]{:S(2)}) %collective-permute-start.3) | collective-permute-done | bytes 16416 | tf_op jit(solution)/shard_map/ppermute | solution.py:350
  13.8 0.9 %shard_map.70.mine_ref = f32[1,40,128]{2,1,0:T(8,128)S(1)} custom-call(f32[640,128]{1,0:T(8,128)S(1)} %get-tuple-element.31.refs_0_, f32[640,128]{1,0:T(8,128)S(1)} %collective-permute-done.1.refs_1_, f32[32,128]{1,0:T(8,128)S(1)} %add.9.refs_2_, f32[32,128]{1,0:T(8,128)S(1)} %collective-permute-done.3.refs_3_, ...), custom_call_target="tpu_custom_call" | custom-call | flops 1000000000 | bytes 1048576 | tf_op jit(solution)/shard_map/pallas_call | solution.py:335
  14.7 2.9 %collective-permute-start.5 = (f32[1,40,128]{2,1,0:T(8,128)S(1)}, f32[1,40,128]{2,1,0:T(8,128)S(1)}, u32[]{:S(2)}, u32[]{:S(2)}) collective-permute-start(f32[1,40,128]{2,1,0:T(8,128)S(1)} %shard_map.70.mine_ref), channel_id=1, source_target_pairs={{0,16},{4,20},{8,24},{12,28},{16,0},{20,4},{24,8},{28,12},{1,17},{... | collective-permute-start | bytes 61448 | tf_op jit(solution)/shard_map/ppermute | solution.py:350
  17.6 1.9 %collective-permute-done.5 = f32[1,40,128]{2,1,0:T(8,128)S(1)} collective-permute-done((f32[1,40,128]{2,1,0:T(8,128)S(1)}, f32[1,40,128]{2,1,0:T(8,128)S(1)}, u32[]{:S(2)}, u32[]{:S(2)}) %collective-permute-start.5) | collective-permute-done | bytes 20512 | tf_op jit(solution)/shard_map/ppermute | solution.py:350
  19.5 1.8 %collective-permute-start.6 = (f32[2,40,128]{2,1,0:T(8,128)S(1)}, f32[2,40,128]{2,1,0:T(8,128)S(1)}, u32[]{:S(2)}, u32[]{:S(2)}) collective-permute-start(f32[2,40,128]{2,1,0:T(8,128)S(1)} %pad_maximum_fusion.2), channel_id=1, source_target_pairs={{0,8},{4,12},{8,0},{12,4},{16,24},{20,28},{24,16},{28,20},{1,9},{5... | collective-permute-start | bytes 122888 | tf_op jit(solution)/shard_map/ppermute | solution.py:350
  21.3 2.2 %collective-permute-done.6 = f32[2,40,128]{2,1,0:T(8,128)S(1)} collective-permute-done((f32[2,40,128]{2,1,0:T(8,128)S(1)}, f32[2,40,128]{2,1,0:T(8,128)S(1)}, u32[]{:S(2)}, u32[]{:S(2)}) %collective-permute-start.6) | collective-permute-done | bytes 40992 | tf_op jit(solution)/shard_map/ppermute | solution.py:350
  23.5 1.7 %collective-permute-start.7 = (f32[4,40,128]{2,1,0:T(8,128)S(1)}, f32[4,40,128]{2,1,0:T(8,128)S(1)}, u32[]{:S(2)}, u32[]{:S(2)}) collective-permute-start(f32[4,40,128]{2,1,0:T(8,128)S(1)} %pad_maximum_fusion.1), channel_id=1, source_target_pairs={{0,4},{4,0},{8,12},{12,8},{16,20},{20,16},{24,28},{28,24},{1,5},{5... | collective-permute-start | bytes 245768 | tf_op jit(solution)/shard_map/ppermute | solution.py:350
  25.2 1.1 %shard_map.71 = (f32[32,256]{1,0:T(8,128)}, f32[132,128]{1,0:T(8,128)S(1)}, f32[132,128]{1,0:T(8,128)S(1)}, f32[32,512]{1,0:T(8,128)S(1)}) custom-call(bf16[256,1024]{1,0:T(8,128)(2,1)S(1)} %get-tuple-element.25.exact_ref, f32[1,40,128]{2,1,0:T(8,128)S(1)} %shard_map.70.mine_ref, f32[1,40,128]{2,1,0:T(8,128)S(1)} %collective-permute-done.4.theirs_ref, ...), custom_call_target="tpu_custom_call" | custom-call | flops 1000000000 | bytes 1048576 | tf_op jit(solution)/shard_map/pallas_call | solution.py:335
  26.6 4.0 %collective-permute-done.9 = f32[132,128]{1,0:T(8,128)S(1)} collective-permute-done((f32[132,128]{1,0:T(8,128)S(1)}, f32[132,128]{1,0:T(8,128)S(1)}, u32[]{:S(2)}, u32[]{:S(2)}) %collective-permute-start.9) | collective-permute-done | bytes 67616 | tf_op jit(solution)/shard_map/ppermute | solution.py:350
  30.6 1.6 %collective-permute-start.10 = (f32[132,128]{1,0:T(8,128)S(1)}, f32[132,128]{1,0:T(8,128)S(1)}, u32[]{:S(2)}, u32[]{:S(2)}) collective-permute-start(f32[132,128]{1,0:T(8,128)S(1)} %add.10), channel_id=1, source_target_pairs={{0,8},{4,12},{8,0},{12,4},{16,24},{20,28},{24,16},{28,20},{1,9},{5... | collective-permute-start | bytes 202760 | tf_op jit(solution)/shard_map/ppermute | solution.py:350
  32.3 2.3 %shard_map.72 = (f32[672,512]{1,0:T(8,128)S(1)}, f32[8,512]{1,0:T(8,128)S(1)}) custom-call(f32[8,40,128]{2,1,0:T(8,128)S(1)} %pad_maximum_fusion.blocks_ref, f32[32,512]{1,0:T(8,128)S(1)} %get-tuple-element.36.vt_ref), custom_call_target="tpu_custom_call" | custom-call | flops 4000000000 | bytes 1048576 | tf_op jit(solution)/shard_map/pallas_call | solution.py:335
  35.0 2.7 %collective-permute-start.11 = (f32[132,128]{1,0:T(8,128)S(1)}, f32[132,128]{1,0:T(8,128)S(1)}, u32[]{:S(2)}, u32[]{:S(2)}) collective-permute-start(f32[132,128]{1,0:T(8,128)S(1)} %add.11.own_ref), channel_id=1, source_target_pairs={{0,16},{4,20},{8,24},{12,28},{16,0},{20,4},{24,8},{28,12},{1,17},{... | collective-permute-start | bytes 202760 | tf_op jit(solution)/shard_map/ppermute | solution.py:350
  37.6 2.3 %shard_map.73 = (f32[672,512]{1,0:T(8,128)S(1)}, f32[8,512]{1,0:T(8,128)S(1)}) custom-call(f32[8,40,128]{2,1,0:T(8,128)S(1)} %collective-permute-done.8.blocks_ref, f32[32,512]{1,0:T(8,128)S(1)} %get-tuple-element.36.vt_ref), custom_call_target="tpu_custom_call" | custom-call | flops 4000000000 | bytes 1048576 | tf_op jit(solution)/shard_map/pallas_call | solution.py:335
  40.0 1.6 %shard_map.74 = (f32[640,512]{1,0:T(8,128)S(1)}, f32[32,512]{1,0:T(8,128)S(1)}) custom-call(f32[672,512]{1,0:T(8,128)S(1)} %get-tuple-element.37.moments_ref, f32[672,512]{1,0:T(8,128)S(1)} %get-tuple-element.38.more_ref), custom_call_target="tpu_custom_call" | custom-call | flops 4000000000 | bytes 1048576 | tf_op jit(solution)/shard_map/pallas_call | solution.py:335
  41.6 0.6 %shard_map.75.own_ref = f32[132,128]{1,0:T(8,128)S(1)} custom-call(f32[640,512]{1,0:T(8,128)S(1)} %get-tuple-element.39.lower_ref, f32[32,512]{1,0:T(8,128)S(1)} %get-tuple-element.40.scale_ref, f32[672,512]{1,0:T(8,128)S(1)} %get-tuple-element.37.moments_ref, f32[672,512]{1,0:T(8,128)S(1)} %get-tuple-element.38.more_ref, ...), custom_call_target="tpu_custom_call" | custom-call | flops 1000000000 | bytes 1048576 | tf_op jit(solution)/shard_map/pallas_call | solution.py:335
  42.8 3.8 %collective-permute-done.12.other_ref = f32[132,128]{1,0:T(8,128)S(1)} collective-permute-done((f32[132,128]{1,0:T(8,128)S(1)}, f32[132,128]{1,0:T(8,128)S(1)}, u32[]{:S(2)}, u32[]{:S(2)}) %collective-permute-start.12) | collective-permute-done | bytes 67616 | tf_op jit(solution)/shard_map/ppermute | solution.py:350
  46.6 0.7 %shard_map.76 = (f32[32,1024]{1,0:T(8,128)}, f32[1,1024]{1,0:T(1,128)}) custom-call(f32[132,128]{1,0:T(8,128)S(1)} %shard_map.75.own_ref, f32[132,128]{1,0:T(8,128)S(1)} %collective-permute-done.12.other_ref), custom_call_target="tpu_custom_call" | custom-call | flops 1000000 | bytes 1048576 | tf_op jit(solution)/shard_map/pallas_call | solution.py:335
  (18 shorter events, 1.9 us)
Async XLA Ops:
  0.6 6.8 %collective-permute-start = (f32[32,1024]{1,0:T(8,128)}, f32[32,1024]{1,0:T(8,128)S(1)}, u32[]{:S(2)}, u32[]{:S(2)}) collective-permute-start(f32[32,1024]{1,0:T(8,128)} %bitcast.6), channel_id=1, source_target_pairs={{0,2},{1,3},{2,0},{3,1},{4,6},{5,7},{6,4},{7,5},{8,10},{9,11},{10,... | collective-permute-start | bytes 393224 | tf_op jit(solution)/shard_map/ppermute | solution.py:350
  8.3 5.5 %collective-permute-start.1 = (f32[640,128]{1,0:T(8,128)S(1)}, f32[640,128]{1,0:T(8,128)S(1)}, u32[]{:S(2)}, u32[]{:S(2)}) collective-permute-start(f32[640,128]{1,0:T(8,128)S(1)} %get-tuple-element.32), channel_id=1, source_target_pairs={{0,1},{1,0},{2,3},{3,2},{4,5},{5,4},{6,7},{7,6},{8,9},{9,8},{10,11... | collective-permute-start | bytes 983048 | tf_op jit(solution)/shard_map/ppermute | solution.py:350
  8.4 1.6 %collective-permute-start.2 = (f32[32,128]{1,0:T(8,128)S(1)}, f32[32,128]{1,0:T(8,128)S(1)}, u32[]{:S(2)}, u32[]{:S(2)}) collective-permute-start(f32[32,128]{1,0:T(8,128)S(1)} %get-tuple-element.34), channel_id=1, source_target_pairs={{0,1},{1,0},{2,3},{3,2},{4,5},{5,4},{6,7},{7,6},{8,9},{9,8},{10,11... | collective-permute-start | bytes 49160 | tf_op jit(solution)/shard_map/ppermute | solution.py:350
  10.1 3.7 %collective-permute-start.3 = (f32[32,128]{1,0:T(8,128)S(1)}, f32[32,128]{1,0:T(8,128)S(1)}, u32[]{:S(2)}, u32[]{:S(2)}) collective-permute-start(f32[32,128]{1,0:T(8,128)S(1)} %add.9.refs_2_), channel_id=1, source_target_pairs={{0,2},{1,3},{2,0},{3,1},{4,6},{5,7},{6,4},{7,5},{8,10},{9,11},{10,... | collective-permute-start | bytes 49160 | tf_op jit(solution)/shard_map/ppermute | solution.py:350
  14.7 4.7 %collective-permute-start.5 = (f32[1,40,128]{2,1,0:T(8,128)S(1)}, f32[1,40,128]{2,1,0:T(8,128)S(1)}, u32[]{:S(2)}, u32[]{:S(2)}) collective-permute-start(f32[1,40,128]{2,1,0:T(8,128)S(1)} %shard_map.70.mine_ref), channel_id=1, source_target_pairs={{0,16},{4,20},{8,24},{12,28},{16,0},{20,4},{24,8},{28,12},{1,17},{... | collective-permute-start | bytes 61448 | tf_op jit(solution)/shard_map/ppermute | solution.py:350
  19.5 4.0 %collective-permute-start.6 = (f32[2,40,128]{2,1,0:T(8,128)S(1)}, f32[2,40,128]{2,1,0:T(8,128)S(1)}, u32[]{:S(2)}, u32[]{:S(2)}) collective-permute-start(f32[2,40,128]{2,1,0:T(8,128)S(1)} %pad_maximum_fusion.2), channel_id=1, source_target_pairs={{0,8},{4,12},{8,0},{12,4},{16,24},{20,28},{24,16},{28,20},{1,9},{5... | collective-permute-start | bytes 122888 | tf_op jit(solution)/shard_map/ppermute | solution.py:350
  21.3 3.9 %collective-permute-start.4 = (f32[1,40,128]{2,1,0:T(8,128)S(1)}, f32[1,40,128]{2,1,0:T(8,128)S(1)}, u32[]{:S(2)}, u32[]{:S(2)}) collective-permute-start(f32[1,40,128]{2,1,0:T(8,128)S(1)} %shard_map.70.mine_ref), channel_id=1, source_target_pairs={{0,1},{1,0},{2,3},{3,2},{4,5},{5,4},{6,7},{7,6},{8,9},{9,8},{10,11... | collective-permute-start | bytes 61448 | tf_op jit(solution)/shard_map/ppermute | solution.py:350
  23.5 8.8 %collective-permute-start.7 = (f32[4,40,128]{2,1,0:T(8,128)S(1)}, f32[4,40,128]{2,1,0:T(8,128)S(1)}, u32[]{:S(2)}, u32[]{:S(2)}) collective-permute-start(f32[4,40,128]{2,1,0:T(8,128)S(1)} %pad_maximum_fusion.1), channel_id=1, source_target_pairs={{0,4},{4,0},{8,12},{12,8},{16,20},{20,16},{24,28},{28,24},{1,5},{5... | collective-permute-start | bytes 245768 | tf_op jit(solution)/shard_map/ppermute | solution.py:350
  26.3 4.3 %collective-permute-start.9 = (f32[132,128]{1,0:T(8,128)S(1)}, f32[132,128]{1,0:T(8,128)S(1)}, u32[]{:S(2)}, u32[]{:S(2)}) collective-permute-start(f32[132,128]{1,0:T(8,128)S(1)} %get-tuple-element.44), channel_id=1, source_target_pairs={{0,4},{4,0},{8,12},{12,8},{16,20},{20,16},{24,28},{28,24},{1,5},{5... | collective-permute-start | bytes 202760 | tf_op jit(solution)/shard_map/ppermute | solution.py:350
  30.6 4.4 %collective-permute-start.10 = (f32[132,128]{1,0:T(8,128)S(1)}, f32[132,128]{1,0:T(8,128)S(1)}, u32[]{:S(2)}, u32[]{:S(2)}) collective-permute-start(f32[132,128]{1,0:T(8,128)S(1)} %add.10), channel_id=1, source_target_pairs={{0,8},{4,12},{8,0},{12,4},{16,24},{20,28},{24,16},{28,20},{1,9},{5... | collective-permute-start | bytes 202760 | tf_op jit(solution)/shard_map/ppermute | solution.py:350
  32.3 5.4 %collective-permute-start.8 = (f32[8,40,128]{2,1,0:T(8,128)S(1)}, f32[8,40,128]{2,1,0:T(8,128)S(1)}, u32[]{:S(2)}, u32[]{:S(2)}) collective-permute-start(f32[8,40,128]{2,1,0:T(8,128)S(1)} %pad_maximum_fusion.blocks_ref), channel_id=1, source_target_pairs={{0,1},{1,0},{2,3},{3,2},{4,5},{5,4},{6,7},{7,6},{8,9},{9,8},{10,11... | collective-permute-start | bytes 491528 | tf_op jit(solution)/shard_map/ppermute | solution.py:350
  35.0 6.7 %collective-permute-start.11 = (f32[132,128]{1,0:T(8,128)S(1)}, f32[132,128]{1,0:T(8,128)S(1)}, u32[]{:S(2)}, u32[]{:S(2)}) collective-permute-start(f32[132,128]{1,0:T(8,128)S(1)} %add.11.own_ref), channel_id=1, source_target_pairs={{0,16},{4,20},{8,24},{12,28},{16,0},{20,4},{24,8},{28,12},{1,17},{... | collective-permute-start | bytes 202760 | tf_op jit(solution)/shard_map/ppermute | solution.py:350
  42.3 4.4 %collective-permute-start.12 = (f32[132,128]{1,0:T(8,128)S(1)}, f32[132,128]{1,0:T(8,128)S(1)}, u32[]{:S(2)}, u32[]{:S(2)}) collective-permute-start(f32[132,128]{1,0:T(8,128)S(1)} %shard_map.75.own_ref), channel_id=1, source_target_pairs={{0,4},{4,0},{8,12},{12,8},{16,20},{20,16},{24,28},{28,24},{1,5},{5... | collective-permute-start | bytes 202760 | tf_op jit(solution)/shard_map/ppermute | solution.py:350

commit v3 on v2

--- a/solution.py
+++ b/solution.py
@@ -56,7 +56,7 @@
     return jnp.concatenate([high, high, mid, high, mid, low, ones], axis=0)
 
 
-def cholesky_columns(get, put, width, lanes):
+def cholesky_columns(get, lower_ref, place, width, lanes):
     blocks = width // SUB
     index = lax.broadcasted_iota(jnp.int32, (SUB, lanes), 0)
     trace = jnp.zeros((SUB, lanes), jnp.float32)
@@ -64,22 +64,25 @@
         trace = trace + jnp.where(index == k % SUB, get(k, k // SUB), 0.0)
     shift = RIDGE + DAMPING / width * jnp.sum(trace, axis=0, keepdims=True)
     scales = []
-    columns = []
     for k in range(width):
         first = k // SUB
         column = {q: get(k, q) for q in range(first, blocks)}
         column[first] = column[first] + jnp.where(index == k % SUB, shift, 0.0)
         for m in range(k):
-            factor = columns[m][first][k % SUB : k % SUB + 1]
+            factor = lower_ref[pl.ds(place[m, first] + k % SUB, SUB, stride=0), :]
             for q in range(first, blocks):
-                column[q] = column[q] - columns[m][q] * factor
+                column[q] = column[q] - lower_ref[place[m, q] : place[m, q] + SUB, :] * factor
         scale = lax.rsqrt(column[first][k % SUB : k % SUB + 1])
-        column = {q: v * scale for q, v in column.items()}
         for q, v in column.items():
-            put(k, q, v)
-        columns.append(column)
+            lower_ref[place[k, q] : place[k, q] + SUB, :] = v * scale
         scales.append(scale)
-    return columns, scales
+    return scales
+
+
+def stored_columns(lower_ref, place, width):
+    return [
+        {q: lower_ref[place[k, q] : place[k, q] + SUB, :] for q in range(k // SUB, width // SUB)} for k in range(width)
+    ]
 
 
 def cholesky_substitute(columns, scales, right, width, lanes):
@@ -138,17 +141,26 @@
         out_ref[...] = lax.dot_general(low, residual, (((1,), (1,)), ((), ())), preferred_element_type=jnp.float32)
 
 
-def factor_moments_kernel(width, add, *refs):
+def factor_moments_kernel(width, step, add, *refs):
     (vt_ref, offset_ref, ut_ref), before, (mine_ref, theirs_ref, table_ref) = refs[:3], refs[3:-3], refs[-3:]
     half = ut_ref.shape[1] // 2
-    vt = vt_ref[...]
-    fill_table(table_ref, vt, width)
+    genes = vt_ref.shape[1]
     left = [stack_left(ut, offset) for ut, offset in zip(halves(ut_ref), halves(offset_ref))]
-    linear = lax.dot_general(
-        stack_right(vt), jnp.concatenate(left, axis=1), (((0,), (0,)), ((), ())), preferred_element_type=jnp.float32
+    left = jnp.concatenate(left, axis=1)
+    chunks = [slice(first, first + step) for first in range(0, genes, step)]
+
+    def weigh(cols):
+        right = stack_right(vt_ref[:, cols])
+        linear = lax.dot_general(right, left, (((0,), (0,)), ((), ())), preferred_element_type=jnp.float32)
+        return jnp.exp(linear).astype(jnp.bfloat16)
+
+    weights = []
+    for cols in chunks:
+        weights.append(weigh(cols))
+        fill_table(table_ref.at[:, cols], vt_ref[:, cols], width)
+    product = sum(
+        jnp.dot(table_ref[:, cols], part, preferred_element_type=jnp.float32) for cols, part in zip(chunks, weights)
     )
-    weights = jnp.exp(linear).astype(jnp.bfloat16)
-    product = jnp.dot(table_ref[...], weights, preferred_element_type=jnp.float32)
     for k, out_ref in enumerate((mine_ref, theirs_ref)):
         total = product[:, k * half : (k + 1) * half]
         if add:
@@ -157,7 +169,7 @@
 
 
 def factor_solve_kernel(width, terms, *refs):
-    moments, (own_ref, other_ref, offset_ref, ut_ref, new_ref) = refs[:terms], refs[terms:]
+    moments, (own_ref, other_ref, offset_ref, ut_ref, new_ref, lower_ref) = refs[:terms], refs[terms:]
     half = own_ref.shape[1]
     place = {piece: SUB * p for p, piece in enumerate(table_pieces(width))}
 
@@ -170,7 +182,8 @@
     for q in range(width // SUB):
         rows = slice(SUB * q, SUB * q + SUB)
         right.append(own_ref[rows] + other_ref[rows] - RIDGE * ut[rows])
-    columns, scales = cholesky_columns(get, lambda a, q, v: None, width, half)
+    scales = cholesky_columns(get, lower_ref, place, width, half)
+    columns = stored_columns(lower_ref, place, width)
     step = cholesky_substitute(columns, scales, right, width, half)
     new_ref[...] = jnp.zeros_like(new_ref)
     for q in range(width // SUB):
@@ -226,53 +239,61 @@
     groups = blocks_ref.shape[0] // per
     rows = SUB * len(table_pieces(width))
     right_ref[...] = stack_right(vt_ref[...])
-    if groups > 1:
-        out_ref[...] = jnp.zeros_like(out_ref)
-        sum_ref[...] = jnp.zeros_like(sum_ref)
-
-    @pl.loop(0, groups)
-    def _(group):
+
+    def prepare(group):
         for b in range(per):
             block = blocks_ref[group * per + b]
             factors = block[:width]
             cols = slice(b * half, (b + 1) * half)
+            left_ref[:, cols] = stack_left(factors, block[width : width + 1])
             fill_table(table_ref.at[:, cols], factors, width)
             table_ref[rows : rows + width, cols] = factors.astype(jnp.bfloat16)
-            left_ref[:, cols] = stack_left(factors, block[width : width + 1])
+
+    def expect(at):
+        linear = lax.dot_general(
+            left_ref[...], right_ref[:, at], (((0,), (0,)), ((), ())), preferred_element_type=jnp.float32
+        )
+        expected = jnp.exp(linear)
+        return jnp.sum(expected, axis=0, keepdims=True), expected.astype(jnp.bfloat16)
+
+    def contract(weights):
+        return jnp.dot(table_ref[...], weights, preferred_element_type=jnp.float32)
+
+    if groups == 1:
+        prepare(0)
+        tiles = [slice(j * tile, (j + 1) * tile) for j in range(genes // tile)]
+        found = [expect(at) for at in tiles]
+        for at, (total, weights) in zip(tiles, found):
+            sum_ref[0:1, at] = total
+            out_ref[:, at] = contract(weights)
+        return
+    out_ref[...] = jnp.zeros_like(out_ref)
+    sum_ref[...] = jnp.zeros_like(sum_ref)
+
+    @pl.loop(0, groups)
+    def _(group):
+        prepare(group)
 
         @pl.loop(0, genes // tile)
         def _(j):
             at = pl.ds(pl.multiple_of(j * tile, tile), tile)
-            linear = lax.dot_general(
-                left_ref[...], right_ref[:, at], (((0,), (0,)), ((), ())), preferred_element_type=jnp.float32
-            )
-            expected = jnp.exp(linear)
-            total = jnp.sum(expected, axis=0, keepdims=True)
-            product = jnp.dot(table_ref[...], expected.astype(jnp.bfloat16), preferred_element_type=jnp.float32)
-            if groups > 1:
-                sum_ref[0:1, at] += total
-                out_ref[:, at] += product
-            else:
-                sum_ref[0:1, at] = total
-                out_ref[:, at] = product
+            total, weights = expect(at)
+            sum_ref[0:1, at] += total
+            out_ref[:, at] += contract(weights)
 
 
 def loading_factor_kernel(width, tile, moments_ref, more_ref, lower_ref, scale_ref):
     genes = moments_ref.shape[1]
     place = {piece: SUB * p for p, piece in enumerate(table_pieces(width))}
 
-    @pl.loop(0, genes // tile)
-    def _(j):
-        at = pl.ds(pl.multiple_of(j * tile, tile), tile)
-
-        def get(a, q):
+    for j in range(genes // tile):
+        at = slice(j * tile, (j + 1) * tile)
+
+        def get(a, q, at=at):
             rows = slice(place[a, q], place[a, q] + SUB)
             return moments_ref[rows, at] + more_ref[rows, at]
 
-        def put(a, q, value):
-            lower_ref[place[a, q] : place[a, q] + SUB, at] = value
-
-        _, scales = cholesky_columns(get, put, width, tile)
+        scales = cholesky_columns(get, lower_ref.at[j], place, width, tile)
         for k in range(width):
             scale_ref[k : k + 1, at] = scales[k]
 
@@ -299,9 +320,7 @@
             expected = expected + more_ref[base + SUB * q : base + SUB * q + SUB, at]
             counted = seen([width * g + SUB * q for g in lanes], SUB)
             right.append(counted - expected - RIDGE * vt_ref[rows, at])
-        columns = [
-            {q: lower_ref[place[k, q] : place[k, q] + SUB, at] for q in range(k // SUB, blocks)} for k in range(width)
-        ]
+        columns = stored_columns(lower_ref.at[j], place, width)
         scales = [scale_ref[k : k + 1, at] for k in range(width)]
         step = cholesky_substitute(columns, scales, right, width, tile)
         fixed = seen([width * groups + g for g in lanes], 1) + sum_ref[0:1, at] + sums_ref[0:1, at]
@@ -387,14 +406,17 @@
     moments = ()
     for k, x in enumerate([vt] + across[1:]):
         moments = kernel_call(
-            functools.partial(factor_moments_kernel, width, k > 0),
+            functools.partial(factor_moments_kernel, width, genes // 2, k > 0),
             (shape((rows, half)), shape((rows, half))),
             [pltpu.VMEM((rows, genes), jnp.bfloat16)],
             10**9,
         )(x, offset, ut, *moments)
     moments = (moments[0], exchange(moments[1], "gene", 1))
     block = kernel_call(
-        functools.partial(factor_solve_kernel, width, len(moments)), shape((1, tall, half)), [], 10**9
+        functools.partial(factor_solve_kernel, width, len(moments)),
+        shape((1, tall, half)),
+        [pltpu.VMEM((rows, half), jnp.float32)],
+        10**9,
     )(*moments, mine, other, offset, ut)
 
     cell_bits = [1 << k for k in range((lax.axis_size("cell") - 1).bit_length())]
@@ -436,15 +458,16 @@
 
     moments, sums = moments_of(gathered)
     more, more_sums = moments_of(opposite)
+    lanes = min(share, 512)
     lower, scales = kernel_call(
-        functools.partial(loading_factor_kernel, width, 256),
-        (shape((rows, share)), shape((width, share))),
+        functools.partial(loading_factor_kernel, width, lanes),
+        (shape((share // lanes, rows, lanes)), shape((width, share))),
         [],
         4 * 10**9,
     )(moments, more)
     total_cells = cells * lax.axis_size("cell")
     result = kernel_call(
-        functools.partial(loading_solve_kernel, width, min(share, 512), total_cells), packed, [], 10**9
+        functools.partial(loading_solve_kernel, width, lanes, total_cells), packed, [], 10**9
     )(lower, scales, moments, more, sums, more_sums, linear, arrived, vt)
     new_loadings, deviance = kernel_call(
         functools.partial(assemble_kernel, width), (shape((width, genes)), shape((1, genes))), [], 10**6

time: 47.5 us -> 46 us (0.968)
  Pallas kernels: 13.1 us -> 10.5 us
  waiting for transfers between devices: 16.4 us -> 17.6 us
    pallas_call x10, Pallas kernels: 13.1 us -> 10.5 us  [call(): pl.pallas_call(body, out_shape=outs, in_specs=[pl.BlockSpec(memory_space=...]
    ppermute x13, waiting for transfers between devices: 16.4 us -> 17.6 us  [exchange(): return lax.ppermute(x, axis, [(i, i ^ bit) for i in range(size)])]
  transfers between devices with their start and end apart: 13 -> 13, of which waited for: 9 -> 8; matrix products, arithmetic and copies ran while one was open for 0% -> 0% of each run, Pallas kernels for 21% -> 16%
where the time goes in v3:
time: 46 us; the launch traced here: 45.9 us
  waiting for transfers between devices  17.6 us (38%)
  starting transfers between devices  17.1 us (37%)
  Pallas kernels  10.5 us (23%)
  between operations  0.72 us (2%)
    ppermute x13, waiting for transfers between devices, exchange(): return lax.ppermute(x, axis, [(i, i ^ bit) for i in range(size)])  17.6 us
    ppermute x13, starting transfers between devices, exchange(): return lax.ppermute(x, axis, [(i, i ^ bit) for i in range(size)])  17.1 us
    pallas_call x10, Pallas kernels, call(): pl.pallas_call(body, out_shape=outs, in_specs=[pl.BlockSpec(memory_space=...  10.5 us
  transfers between devices with their start and end apart: 13, of which 8 were waited for; matrix products, arithmetic and copies ran while one was open for 0% of the time, Pallas kernels for 16%

profile of v3, /device:TPU:0, one launch (start us, length us, event | category | flops | bytes accessed | tf_op | source)
XLA Modules:
  0.0 45.9 jit_solution(17412267842748431187)
XLA Ops:
  0.6 3.1 %collective-permute-start = (f32[32,1024]{1,0:T(8,128)}, f32[32,1024]{1,0:T(8,128)S(1)}, u32[]{:S(2)}, u32[]{:S(2)}) collective-permute-start(f32[32,1024]{1,0:T(8,128)} %bitcast.6), channel_id=1, source_target_pairs={{0,2},{1,3},{2,0},{3,1},{4,6},{5,7},{6,4},{7,5},{8,10},{9,11},{10,... | collective-permute-start | bytes 393224 | tf_op jit(solution)/shard_map/ppermute | solution.py:369
  3.7 1.7 %shard_map.67 = (f32[32,128]{1,0:T(8,128)S(1)}, f32[32,128]{1,0:T(8,128)S(1)}, bf16[256,1024]{1,0:T(8,128)(2,1)S(1)}, f32[1,256]{1,0:T(1,128)S(1)}, f32[32,256]{1,0:T(8,128)S(1)}, /*index=5*/f32[32,1024]{1,0:T(8,128)S(1)}) custom-call(s32[256,1024]{1,0:T(8,128)} %counts_hbm.1, s32[1,256]{1,0:T(1,128)} %bitcast.11, f32[32,256]{1,0:T(8,128)} %bitcast.9, ...), custom_call_target="tpu_custom_call" | custom-call | flops 1000000000 | bytes 1048576 | tf_op jit(solution)/shard_map/pallas_call | solution.py:354
  5.4 0.8 %shard_map.68 = (f32[640,128]{1,0:T(8,128)S(1)}, f32[640,128]{1,0:T(8,128)S(1)}) custom-call(f32[32,1024]{1,0:T(8,128)S(1)} %get-tuple-element.28.refs_0_.vt_ref, f32[1,256]{1,0:T(1,128)S(1)} %get-tuple-element.26.refs_1_.refs_4_, f32[32,256]{1,0:T(8,128)S(1)} %get-tuple-element.27.refs_2_.refs_5_), custom_call_target="tpu_custom_call" | custom-call | flops 1000000000 | bytes 1048576 | tf_op jit(solution)/shard_map/pallas_call | solution.py:354
  6.2 1.2 %collective-permute-done.refs_0_ = f32[32,1024]{1,0:T(8,128)S(1)} collective-permute-done((f32[32,1024]{1,0:T(8,128)}, f32[32,1024]{1,0:T(8,128)S(1)}, u32[]{:S(2)}, u32[]{:S(2)}) %collective-permute-start) | collective-permute-done | bytes 131104 | tf_op jit(solution)/shard_map/ppermute | solution.py:369
  7.4 0.8 %shard_map.69 = (f32[640,128]{1,0:T(8,128)S(1)}, f32[640,128]{1,0:T(8,128)S(1)}) custom-call(f32[32,1024]{1,0:T(8,128)S(1)} %collective-permute-done.refs_0_, f32[1,256]{1,0:T(1,128)S(1)} %get-tuple-element.26.refs_1_.refs_4_, f32[32,256]{1,0:T(8,128)S(1)} %get-tuple-element.27.refs_2_.refs_5_, f32[640,128]{1,0:T(8,128)S(1)} %get-tuple-element.29.refs_3_, ...), custom_call_target="tpu_custom_call" | custom-call | flops 1000000000 | bytes 1048576 | tf_op jit(solution)/shard_map/pallas_call | solution.py:354
  8.8 1.1 %collective-permute-done.2 = f32[32,128]{1,0:T(8,128)S(1)} collective-permute-done((f32[32,128]{1,0:T(8,128)S(1)}, f32[32,128]{1,0:T(8,128)S(1)}, u32[]{:S(2)}, u32[]{:S(2)}) %collective-permute-start.2) | collective-permute-done | bytes 16416 | tf_op jit(solution)/shard_map/ppermute | solution.py:369
  9.9 1.7 %collective-permute-start.3 = (f32[32,128]{1,0:T(8,128)S(1)}, f32[32,128]{1,0:T(8,128)S(1)}, u32[]{:S(2)}, u32[]{:S(2)}) collective-permute-start(f32[32,128]{1,0:T(8,128)S(1)} %add.9.refs_2_), channel_id=1, source_target_pairs={{0,2},{1,3},{2,0},{3,1},{4,6},{5,7},{6,4},{7,5},{8,10},{9,11},{10,... | collective-permute-start | bytes 49160 | tf_op jit(solution)/shard_map/ppermute | solution.py:369
  11.7 2.0 %collective-permute-done.3.refs_3_ = f32[32,128]{1,0:T(8,128)S(1)} collective-permute-done((f32[32,128]{1,0:T(8,128)S(1)}, f32[32,128]{1,0:T(8,128)S(1)}, u32[]{:S(2)}, u32[]{:S(2)}) %collective-permute-start.3) | collective-permute-done | bytes 16416 | tf_op jit(solution)/shard_map/ppermute | solution.py:369
  13.7 1.0 %shard_map.70.mine_ref = f32[1,40,128]{2,1,0:T(8,128)S(1)} custom-call(f32[640,128]{1,0:T(8,128)S(1)} %get-tuple-element.31.refs_0_, f32[640,128]{1,0:T(8,128)S(1)} %collective-permute-done.1.refs_1_, f32[32,128]{1,0:T(8,128)S(1)} %add.9.refs_2_, f32[32,128]{1,0:T(8,128)S(1)} %collective-permute-done.3.refs_3_, ...), custom_call_target="tpu_custom_call" | custom-call | flops 1000000000 | bytes 1048576 | tf_op jit(solution)/shard_map/pallas_call | solution.py:354
  14.6 2.9 %collective-permute-start.5 = (f32[1,40,128]{2,1,0:T(8,128)S(1)}, f32[1,40,128]{2,1,0:T(8,128)S(1)}, u32[]{:S(2)}, u32[]{:S(2)}) collective-permute-start(f32[1,40,128]{2,1,0:T(8,128)S(1)} %shard_map.70.mine_ref), channel_id=1, source_target_pairs={{0,16},{4,20},{8,24},{12,28},{16,0},{20,4},{24,8},{28,12},{1,17},{... | collective-permute-start | bytes 61448 | tf_op jit(solution)/shard_map/ppermute | solution.py:369
  17.5 1.9 %collective-permute-done.5 = f32[1,40,128]{2,1,0:T(8,128)S(1)} collective-permute-done((f32[1,40,128]{2,1,0:T(8,128)S(1)}, f32[1,40,128]{2,1,0:T(8,128)S(1)}, u32[]{:S(2)}, u32[]{:S(2)}) %collective-permute-start.5) | collective-permute-done | bytes 20512 | tf_op jit(solution)/shard_map/ppermute | solution.py:369
  19.4 1.8 %collective-permute-start.6 = (f32[2,40,128]{2,1,0:T(8,128)S(1)}, f32[2,40,128]{2,1,0:T(8,128)S(1)}, u32[]{:S(2)}, u32[]{:S(2)}) collective-permute-start(f32[2,40,128]{2,1,0:T(8,128)S(1)} %pad_maximum_fusion.2), channel_id=1, source_target_pairs={{0,8},{4,12},{8,0},{12,4},{16,24},{20,28},{24,16},{28,20},{1,9},{5... | collective-permute-start | bytes 122888 | tf_op jit(solution)/shard_map/ppermute | solution.py:369
  21.2 2.2 %collective-permute-done.6 = f32[2,40,128]{2,1,0:T(8,128)S(1)} collective-permute-done((f32[2,40,128]{2,1,0:T(8,128)S(1)}, f32[2,40,128]{2,1,0:T(8,128)S(1)}, u32[]{:S(2)}, u32[]{:S(2)}) %collective-permute-start.6) | collective-permute-done | bytes 40992 | tf_op jit(solution)/shard_map/ppermute | solution.py:369
  23.4 1.7 %collective-permute-start.7 = (f32[4,40,128]{2,1,0:T(8,128)S(1)}, f32[4,40,128]{2,1,0:T(8,128)S(1)}, u32[]{:S(2)}, u32[]{:S(2)}) collective-permute-start(f32[4,40,128]{2,1,0:T(8,128)S(1)} %pad_maximum_fusion.1), channel_id=1, source_target_pairs={{0,4},{4,0},{8,12},{12,8},{16,20},{20,16},{24,28},{28,24},{1,5},{5... | collective-permute-start | bytes 245768 | tf_op jit(solution)/shard_map/ppermute | solution.py:369
  25.1 1.1 %shard_map.71 = (f32[32,256]{1,0:T(8,128)}, f32[132,128]{1,0:T(8,128)S(1)}, f32[132,128]{1,0:T(8,128)S(1)}, f32[32,512]{1,0:T(8,128)S(1)}) custom-call(bf16[256,1024]{1,0:T(8,128)(2,1)S(1)} %get-tuple-element.25.exact_ref, f32[1,40,128]{2,1,0:T(8,128)S(1)} %shard_map.70.mine_ref, f32[1,40,128]{2,1,0:T(8,128)S(1)} %collective-permute-done.4.theirs_ref, ...), custom_call_target="tpu_custom_call" | custom-call | flops 1000000000 | bytes 1048576 | tf_op jit(solution)/shard_map/pallas_call | solution.py:354
  26.5 4.0 %collective-permute-done.9 = f32[132,128]{1,0:T(8,128)S(1)} collective-permute-done((f32[132,128]{1,0:T(8,128)S(1)}, f32[132,128]{1,0:T(8,128)S(1)}, u32[]{:S(2)}, u32[]{:S(2)}) %collective-permute-start.9) | collective-permute-done | bytes 67616 | tf_op jit(solution)/shard_map/ppermute | solution.py:369
  30.5 1.6 %collective-permute-start.10 = (f32[132,128]{1,0:T(8,128)S(1)}, f32[132,128]{1,0:T(8,128)S(1)}, u32[]{:S(2)}, u32[]{:S(2)}) collective-permute-start(f32[132,128]{1,0:T(8,128)S(1)} %add.10), channel_id=1, source_target_pairs={{0,8},{4,12},{8,0},{12,4},{16,24},{20,28},{24,16},{28,20},{1,9},{5... | collective-permute-start | bytes 202760 | tf_op jit(solution)/shard_map/ppermute | solution.py:369
  32.2 1.3 %shard_map.72 = (f32[672,512]{1,0:T(8,128)S(1)}, f32[8,512]{1,0:T(8,128)S(1)}) custom-call(f32[8,40,128]{2,1,0:T(8,128)S(1)} %pad_maximum_fusion.blocks_ref, f32[32,512]{1,0:T(8,128)S(1)} %get-tuple-element.36.vt_ref), custom_call_target="tpu_custom_call" | custom-call | flops 4000000000 | bytes 1048576 | tf_op jit(solution)/shard_map/pallas_call | solution.py:354
  33.5 1.4 %collective-permute-done.10 = f32[132,128]{1,0:T(8,128)S(1)} collective-permute-done((f32[132,128]{1,0:T(8,128)S(1)}, f32[132,128]{1,0:T(8,128)S(1)}, u32[]{:S(2)}, u32[]{:S(2)}) %collective-permute-start.10) | collective-permute-done | bytes 67616 | tf_op jit(solution)/shard_map/ppermute | solution.py:369
  34.9 2.7 %collective-permute-start.11 = (f32[132,128]{1,0:T(8,128)S(1)}, f32[132,128]{1,0:T(8,128)S(1)}, u32[]{:S(2)}, u32[]{:S(2)}) collective-permute-start(f32[132,128]{1,0:T(8,128)S(1)} %add.11.own_ref), channel_id=1, source_target_pairs={{0,16},{4,20},{8,24},{12,28},{16,0},{20,4},{24,8},{28,12},{1,17},{... | collective-permute-start | bytes 202760 | tf_op jit(solution)/shard_map/ppermute | solution.py:369
  37.6 1.3 %shard_map.73 = (f32[672,512]{1,0:T(8,128)S(1)}, f32[8,512]{1,0:T(8,128)S(1)}) custom-call(f32[8,40,128]{2,1,0:T(8,128)S(1)} %collective-permute-done.8.blocks_ref, f32[32,512]{1,0:T(8,128)S(1)} %get-tuple-element.36.vt_ref), custom_call_target="tpu_custom_call" | custom-call | flops 4000000000 | bytes 1048576 | tf_op jit(solution)/shard_map/pallas_call | solution.py:354
  38.8 1.3 %shard_map.74 = (f32[1,640,512]{2,1,0:T(8,128)S(1)}, f32[32,512]{1,0:T(8,128)S(1)}) custom-call(f32[672,512]{1,0:T(8,128)S(1)} %get-tuple-element.37.moments_ref, f32[672,512]{1,0:T(8,128)S(1)} %get-tuple-element.38.more_ref), custom_call_target="tpu_custom_call" | custom-call | flops 4000000000 | bytes 1048576 | tf_op jit(solution)/shard_map/pallas_call | solution.py:354
  41.4 3.8 %collective-permute-done.12.other_ref = f32[132,128]{1,0:T(8,128)S(1)} collective-permute-done((f32[132,128]{1,0:T(8,128)S(1)}, f32[132,128]{1,0:T(8,128)S(1)}, u32[]{:S(2)}, u32[]{:S(2)}) %collective-permute-start.12) | collective-permute-done | bytes 67616 | tf_op jit(solution)/shard_map/ppermute | solution.py:369
  45.2 0.7 %shard_map.76 = (f32[32,1024]{1,0:T(8,128)}, f32[1,1024]{1,0:T(1,128)}) custom-call(f32[132,128]{1,0:T(8,128)S(1)} %shard_map.75.own_ref, f32[132,128]{1,0:T(8,128)S(1)} %collective-permute-done.12.other_ref), custom_call_target="tpu_custom_call" | custom-call | flops 1000000 | bytes 1048576 | tf_op jit(solution)/shard_map/pallas_call | solution.py:354
  (18 shorter events, 2.3 us)
Async XLA Ops:
  0.6 6.8 %collective-permute-start = (f32[32,1024]{1,0:T(8,128)}, f32[32,1024]{1,0:T(8,128)S(1)}, u32[]{:S(2)}, u32[]{:S(2)}) collective-permute-start(f32[32,1024]{1,0:T(8,128)} %bitcast.6), channel_id=1, source_target_pairs={{0,2},{1,3},{2,0},{3,1},{4,6},{5,7},{6,4},{7,5},{8,10},{9,11},{10,... | collective-permute-start | bytes 393224 | tf_op jit(solution)/shard_map/ppermute | solution.py:369
  8.2 5.5 %collective-permute-start.1 = (f32[640,128]{1,0:T(8,128)S(1)}, f32[640,128]{1,0:T(8,128)S(1)}, u32[]{:S(2)}, u32[]{:S(2)}) collective-permute-start(f32[640,128]{1,0:T(8,128)S(1)} %get-tuple-element.32), channel_id=1, source_target_pairs={{0,1},{1,0},{2,3},{3,2},{4,5},{5,4},{6,7},{7,6},{8,9},{9,8},{10,11... | collective-permute-start | bytes 983048 | tf_op jit(solution)/shard_map/ppermute | solution.py:369
  8.3 1.6 %collective-permute-start.2 = (f32[32,128]{1,0:T(8,128)S(1)}, f32[32,128]{1,0:T(8,128)S(1)}, u32[]{:S(2)}, u32[]{:S(2)}) collective-permute-start(f32[32,128]{1,0:T(8,128)S(1)} %get-tuple-element.34), channel_id=1, source_target_pairs={{0,1},{1,0},{2,3},{3,2},{4,5},{5,4},{6,7},{7,6},{8,9},{9,8},{10,11... | collective-permute-start | bytes 49160 | tf_op jit(solution)/shard_map/ppermute | solution.py:369
  9.9 3.7 %collective-permute-start.3 = (f32[32,128]{1,0:T(8,128)S(1)}, f32[32,128]{1,0:T(8,128)S(1)}, u32[]{:S(2)}, u32[]{:S(2)}) collective-permute-start(f32[32,128]{1,0:T(8,128)S(1)} %add.9.refs_2_), channel_id=1, source_target_pairs={{0,2},{1,3},{2,0},{3,1},{4,6},{5,7},{6,4},{7,5},{8,10},{9,11},{10,... | collective-permute-start | bytes 49160 | tf_op jit(solution)/shard_map/ppermute | solution.py:369
  14.6 4.7 %collective-permute-start.5 = (f32[1,40,128]{2,1,0:T(8,128)S(1)}, f32[1,40,128]{2,1,0:T(8,128)S(1)}, u32[]{:S(2)}, u32[]{:S(2)}) collective-permute-start(f32[1,40,128]{2,1,0:T(8,128)S(1)} %shard_map.70.mine_ref), channel_id=1, source_target_pairs={{0,16},{4,20},{8,24},{12,28},{16,0},{20,4},{24,8},{28,12},{1,17},{... | collective-permute-start | bytes 61448 | tf_op jit(solution)/shard_map/ppermute | solution.py:369
  19.4 4.0 %collective-permute-start.6 = (f32[2,40,128]{2,1,0:T(8,128)S(1)}, f32[2,40,128]{2,1,0:T(8,128)S(1)}, u32[]{:S(2)}, u32[]{:S(2)}) collective-permute-start(f32[2,40,128]{2,1,0:T(8,128)S(1)} %pad_maximum_fusion.2), channel_id=1, source_target_pairs={{0,8},{4,12},{8,0},{12,4},{16,24},{20,28},{24,16},{28,20},{1,9},{5... | collective-permute-start | bytes 122888 | tf_op jit(solution)/shard_map/ppermute | solution.py:369
  21.2 3.9 %collective-permute-start.4 = (f32[1,40,128]{2,1,0:T(8,128)S(1)}, f32[1,40,128]{2,1,0:T(8,128)S(1)}, u32[]{:S(2)}, u32[]{:S(2)}) collective-permute-start(f32[1,40,128]{2,1,0:T(8,128)S(1)} %shard_map.70.mine_ref), channel_id=1, source_target_pairs={{0,1},{1,0},{2,3},{3,2},{4,5},{5,4},{6,7},{7,6},{8,9},{9,8},{10,11... | collective-permute-start | bytes 61448 | tf_op jit(solution)/shard_map/ppermute | solution.py:369
  23.4 8.8 %collective-permute-start.7 = (f32[4,40,128]{2,1,0:T(8,128)S(1)}, f32[4,40,128]{2,1,0:T(8,128)S(1)}, u32[]{:S(2)}, u32[]{:S(2)}) collective-permute-start(f32[4,40,128]{2,1,0:T(8,128)S(1)} %pad_maximum_fusion.1), channel_id=1, source_target_pairs={{0,4},{4,0},{8,12},{12,8},{16,20},{20,16},{24,28},{28,24},{1,5},{5... | collective-permute-start | bytes 245768 | tf_op jit(solution)/shard_map/ppermute | solution.py:369
  26.2 4.3 %collective-permute-start.9 = (f32[132,128]{1,0:T(8,128)S(1)}, f32[132,128]{1,0:T(8,128)S(1)}, u32[]{:S(2)}, u32[]{:S(2)}) collective-permute-start(f32[132,128]{1,0:T(8,128)S(1)} %get-tuple-element.44), channel_id=1, source_target_pairs={{0,4},{4,0},{8,12},{12,8},{16,20},{20,16},{24,28},{28,24},{1,5},{5... | collective-permute-start | bytes 202760 | tf_op jit(solution)/shard_map/ppermute | solution.py:369
  30.5 4.4 %collective-permute-start.10 = (f32[132,128]{1,0:T(8,128)S(1)}, f32[132,128]{1,0:T(8,128)S(1)}, u32[]{:S(2)}, u32[]{:S(2)}) collective-permute-start(f32[132,128]{1,0:T(8,128)S(1)} %add.10), channel_id=1, source_target_pairs={{0,8},{4,12},{8,0},{12,4},{16,24},{20,28},{24,16},{28,20},{1,9},{5... | collective-permute-start | bytes 202760 | tf_op jit(solution)/shard_map/ppermute | solution.py:369
  32.2 5.4 %collective-permute-start.8 = (f32[8,40,128]{2,1,0:T(8,128)S(1)}, f32[8,40,128]{2,1,0:T(8,128)S(1)}, u32[]{:S(2)}, u32[]{:S(2)}) collective-permute-start(f32[8,40,128]{2,1,0:T(8,128)S(1)} %pad_maximum_fusion.blocks_ref), channel_id=1, source_target_pairs={{0,1},{1,0},{2,3},{3,2},{4,5},{5,4},{6,7},{7,6},{8,9},{9,8},{10,11... | collective-permute-start | bytes 491528 | tf_op jit(solution)/shard_map/ppermute | solution.py:369
  34.9 5.3 %collective-permute-start.11 = (f32[132,128]{1,0:T(8,128)S(1)}, f32[132,128]{1,0:T(8,128)S(1)}, u32[]{:S(2)}, u32[]{:S(2)}) collective-permute-start(f32[132,128]{1,0:T(8,128)S(1)} %add.11.own_ref), channel_id=1, source_target_pairs={{0,16},{4,20},{8,24},{12,28},{16,0},{20,4},{24,8},{28,12},{1,17},{... | collective-permute-start | bytes 202760 | tf_op jit(solution)/shard_map/ppermute | solution.py:369
  40.8 4.4 %collective-permute-start.12 = (f32[132,128]{1,0:T(8,128)S(1)}, f32[132,128]{1,0:T(8,128)S(1)}, u32[]{:S(2)}, u32[]{:S(2)}) collective-permute-start(f32[132,128]{1,0:T(8,128)S(1)} %shard_map.75.own_ref), channel_id=1, source_target_pairs={{0,4},{4,0},{8,12},{12,8},{16,20},{20,16},{24,28},{28,24},{1,5},{5... | collective-permute-start | bytes 202760 | tf_op jit(solution)/shard_map/ppermute | solution.py:369
